TPU v7x, 32 devices: a whole 2x2x4 slice. The times are simulated.
32 devices in a mesh: parts: 2 (over y), seq: 4 (over z), tok: 2 (over x), head: 2 (over core).
Axes of the slice: x: 2, y: 2, z: 4, core: 2. Of those that a mesh axis runs over, the one named last changes fastest.
Arguments:
- values: bfloat16 [8192, 2048], P(('parts', 'seq', 'tok'), 'head'), parts along dimension 0, may hold values from -6 to 6
- key_rows: bfloat16 [8192, 128], P(('parts', 'seq', 'tok')), parts along dimension 0, may hold values from -0.5 to 0.5
- query_rows: bfloat16 [8192, 128], P(('parts', 'seq', 'tok')), parts along dimension 0, may hold values from -6 to 6
- decay_codes: int32 [32, 8192], P('head', ('parts', 'seq', 'tok')), parts along dimension 1, may hold values from 0 to 48398, as said below
- weight_codes: int32 [12, 32, 8192], P(None, 'head', ('parts', 'seq', 'tok')), parts along dimension 2, may hold values from 16 to 511
- norm_gain: float32 [2048], P('head'), may hold values from 0.5 to 1.5
Outputs:
- mixed: bfloat16 [8192, 2048], P(('parts', 'seq', 'tok'), 'head'), parts along dimension 0
There are 2 independent parts, one for each index of `parts`. A program takes and returns all parts, laid end to end along the dimension named above; an argument that names none is the same for every part. Nothing has to cross between parts.
Inputs may be any that keep to these rules, and one draw needn't show every extreme that they name: `decay_codes`: Log-decay numerators over 65536. `weight_codes`: level weight numerators over 256.
All inputs are finite; a program needn't handle non-finite values.
Results may differ from a plain program's by a relative error of at most 0.0048.
Values sent between devices are 32-bit elements; how exact they have to be, the bound alone decides.
No kernel may reach another device: no remote copies, remote signals or barrier semaphores. Data moves between devices by JAX's collectives and lax.ppermute only.
A program may use at most 64 MiB of HBM per device.

v0:
```python
import jax
import jax.numpy as jnp
from jax import lax
from jax.sharding import PartitionSpec as P

BUCKET = 64


decay_denominator = 65536.0
weight_denominator = 256.0
norm_epsilon = 1e-05
row_limit = 512
highest = lax.Precision.HIGHEST


def from_partner(value, axis, distance):
    mask = 2**distance
    pairs = [(source, source ^ mask) for source in range(lax.axis_size(axis))]
    return lax.ppermute(value, axis, pairs)


def bit_count(numbers, width_bits):
    result = jnp.zeros(numbers.shape, jnp.int32)
    for bit_place in range(width_bits):
        result = result + (numbers >= 1 << bit_place).astype(jnp.int32)
    return result


def token_spread(levels_full, lam_rows, slot_count):
    spread = jnp.zeros(levels_full.shape, jnp.float32)
    for slot in range(slot_count):
        spread = spread + jnp.where(levels_full == slot, lam_rows[slot][:, None], 0.0)
    return spread


def decay_sums(decay_codes):
    return jnp.cumsum(-decay_codes.astype(jnp.float32) / decay_denominator, axis=1)


def near_terms(values, key_rows, query_rows, cumulative, level_scale, head_size):
    token_count = values.shape[0]
    head_count = cumulative.shape[0]
    buckets = token_count // BUCKET
    level_bits = (buckets - 1).bit_length()
    bucket_ids = jnp.arange(buckets, dtype=jnp.int32)
    levels = bit_count(jnp.bitwise_xor(bucket_ids[:, None], bucket_ids[None, :]), level_bits)
    head_weights = jnp.transpose(level_scale[: level_bits + 1], (1, 0, 2))
    block_rows = min(row_limit, token_count)
    scores = jnp.einsum("tn,sn->ts", query_rows, key_rows, preferred_element_type=jnp.float32)
    causal = jnp.arange(0, block_rows)[:, None] >= jnp.arange(block_rows)[None, :]
    levels_full = jnp.broadcast_to(
        levels[:, None, :, None], (block_rows // BUCKET, BUCKET, block_rows // BUCKET, BUCKET)
    ).reshape(block_rows, block_rows)

    def one_head(head_item):
        cum_rates, weights, head_index = head_item
        log_gap = jnp.where(
            causal, cum_rates[0:block_rows, None] - cum_rates[None, :block_rows], 0.0
        )
        spread = token_spread(levels_full, weights, level_bits + 1)
        mixing = jnp.where(causal, jnp.exp(log_gap) * spread * scores, 0.0).astype(jnp.bfloat16)
        columns = lax.dynamic_slice_in_dim(values, head_index * head_size, head_size, 1)
        return jnp.dot(mixing, columns, preferred_element_type=jnp.float32)

    pieces = lax.map(one_head, (cumulative, head_weights, jnp.arange(head_count, dtype=jnp.int32)))
    return pieces


def block_state(values, key_rows, cumulative, head_size):
    token_count = values.shape[0]
    head_count = cumulative.shape[0]
    end_decay = jnp.exp(cumulative[:, -1:] - cumulative)
    decayed = (
        values.astype(jnp.float32).reshape(token_count, head_count, head_size)
        * end_decay.T[:, :, None]
    ).astype(jnp.bfloat16)
    return jnp.einsum("tn,thp->hnp", key_rows, decayed, preferred_element_type=jnp.float32)


def decay_coeff(sources, own_index, log_gap):
    earlier = (sources < own_index)[:, None]
    return jnp.where(earlier, jnp.exp(jnp.where(earlier, log_gap, 0.0)), 0.0)


def level_onehot(levels, slot_ids):
    return (levels[:, None] == slot_ids[None, :]).astype(jnp.float32)


def pair_step(aggregate, block_total, prefix, far_levels, slot, partner, partner_total, is_upper):
    weight = jnp.where(is_upper, jnp.exp(prefix), 0.0)
    far_levels = far_levels.at[slot].add(weight[:, None, None] * partner)
    aggregate = jnp.where(
        is_upper,
        jnp.exp(block_total)[:, None, None] * partner + aggregate,
        jnp.exp(partner_total)[:, None, None] * aggregate + partner,
    )
    prefix = jnp.where(is_upper, prefix + partner_total, prefix)
    return (aggregate, block_total + partner_total, prefix, far_levels)


def finish(near, far_levels, far_weights, query_rows, cumulative, norm_gain, head_size):
    token_count = query_rows.shape[0]
    head_count = cumulative.shape[0]
    queries = query_rows.astype(jnp.float32)
    readout = jnp.zeros(near.shape, jnp.float32)
    for slot in range(far_levels.shape[0]):
        part_out = jnp.einsum("tn,hnp->htp", queries, far_levels[slot], precision=highest)
        readout = readout + far_weights[slot][:, :, None] * part_out
    combined = near + jnp.exp(cumulative)[:, :, None] * readout
    inverse_rms = lax.rsqrt(jnp.mean(combined * combined, axis=2, keepdims=True) + norm_epsilon)
    normed = combined * inverse_rms * norm_gain.reshape(head_count, 1, head_size)
    return (
        jnp.transpose(normed, (1, 0, 2))
        .reshape(token_count, head_count * head_size)
        .astype(jnp.bfloat16)
    )


def local(values, key_rows, query_rows, decay_codes, weight_codes, norm_gain):
    head_count = decay_codes.shape[0]
    head_size = values.shape[1] // head_count
    level_scale = weight_codes.astype(jnp.float32) / weight_denominator
    cumulative = decay_sums(decay_codes)
    own_state = block_state(values, key_rows, cumulative, head_size)
    near = near_terms(values, key_rows, query_rows, cumulative, level_scale, head_size)
    base_level = (values.shape[0] // BUCKET).bit_length() - 1
    tok_count = lax.axis_size("tok")
    tok_bits = tok_count.bit_length() - 1
    tok_index = lax.axis_index("tok")
    seq_count = lax.axis_size("seq")
    seq_bits = seq_count.bit_length() - 1
    seq_index = lax.axis_index("seq")
    far_levels = jnp.zeros((tok_bits + seq_bits,) + own_state.shape, jnp.float32)
    aggregate = own_state
    block_total = cumulative[:, -1]
    prefix = jnp.zeros(block_total.shape, jnp.float32)
    for bit_place in range(tok_bits):
        partner, partner_total = from_partner((aggregate, block_total), "tok", bit_place)
        is_upper = tok_index >> bit_place & 1 == 1
        aggregate, block_total, prefix, far_levels = pair_step(
            aggregate, block_total, prefix, far_levels, bit_place, partner, partner_total, is_upper
        )
    totals = lax.all_gather(block_total[None], "seq", axis=0, tiled=True)
    inclusive = jnp.cumsum(totals, axis=0)
    before_me = jnp.sum(
        jnp.where((jnp.arange(seq_count, dtype=jnp.int32) < seq_index)[:, None], totals, 0.0),
        axis=0,
    )
    reach = prefix + before_me
    seq_slots = jnp.arange(1, seq_bits + 1, dtype=jnp.int32)
    shard_piece = lax.all_gather(aggregate[None], "seq", axis=0, tiled=True)
    sources = jnp.arange(shard_piece.shape[0], dtype=jnp.int32)
    coefficient = decay_coeff(sources, seq_index, reach[None, :] - inclusive)
    onehot = level_onehot(bit_count(jnp.bitwise_xor(sources, seq_index), seq_bits), seq_slots)
    added = jnp.einsum("mh,mj,mhnp->jhnp", coefficient, onehot, shard_piece, precision=highest)
    far_levels = far_levels.at[tok_bits:].add(added)
    far_weights = level_scale[base_level + 1 : base_level + 1 + tok_bits + seq_bits]
    return finish(near, far_levels, far_weights, query_rows, cumulative, norm_gain, head_size)


def solution(mesh):
    return jax.shard_map(
        local,
        mesh=mesh,
        in_specs=(
            P(("parts", "seq", "tok"), "head"),
            P(("parts", "seq", "tok"), None),
            P(("parts", "seq", "tok"), None),
            P("head", ("parts", "seq", "tok")),
            P(None, "head", ("parts", "seq", "tok")),
            P("head"),
        ),
        out_specs=P(("parts", "seq", "tok"), "head"),
        check_vma=False,
    )
```

profile of v0, /device:TPU:0, one launch (start us, length us, event | category | flops | bytes accessed | tf_op | source)
XLA Modules:
  0.0 126.6 jit_solution(5198924465103910711)
XLA Ops:
  6.5 0.8 copy_bitcast_fusion.1
  7.4 1.1 reduce-window.6
  9.0 3.0 %collective-permute-start.1 = (f32[16]{0:T(128)S(1)}, f32[16]{0:T(128)S(1)}, u32[]{:S(2)}, u32[]{:S(2)}) collective-permute-start(f32[16]{0:T(128)S(1)} %slice_reduce_fusion.1), channel_id=1, source_target_pairs={{0,2},{2,0},{1,3},{3,1},{4,6},{6,4},{5,7},{7,5},{8,10},{10,8},{9,1... | collective-permute-start | bytes 200 | tf_op jit(solution)/shard_map/ppermute | solution.py:19
  12.1 1.5 %copy.29 = bf16[512,1024]{0,1:T(8,128)(2,1)S(1)} copy(bf16[512,1024]{1,0:T(8,128)(2,1)} %param.12) | data formatting | bytes 2097152 | tf_op args[0]
  14.5 0.8 copy-done.4
  15.3 1.3 %fusion.58 = f32[512,512]{1,0:T(8,128)} fusion(bf16[512,128]{1,0:T(8,128)(2,1)S(1)} %copy-done, bf16[512,128]{1,0:T(8,128)(2,1)S(1)} %copy-done.5), kind=kOutput, calls=%fused_computation.89 | convolution fusion | flops 67108864 | bytes 1310720 | tf_op jit(solution)/shard_map/tn,sn->ts/dot_general | solution.py:49
  17.8 12.4 %all-reduce = f32[64]{0:T(128)S(1)} all-reduce(f32[64]{0:T(128)S(1)} %get-tuple-element.165), channel_id=2, replica_groups=mesh['parts'=2,'seq'=4,'tok'=2,'head'=2] {'seq'}, use_global_device_ids=true, to_apply=%add | all-reduce | flops 64 | bytes 512
  30.4 1.0 add_select_fusion
  31.5 73.4 %while.14 = (s32[]{:T(128)}, f32[16,512,64]{1,2,0:T(8,128)}, f32[16,512]{1,0:T(8,128)S(1)}, f32[16,4,512]{2,1,0:T(4,128)S(1)}, f32[512,512]{1,0:T(8,128)}, /*ind...) while((s32[]{:T(128)}, f32[16,512,64]{1,2,0:T(8,128)}, ...), condition=%wide.region_3.4_spmd.clone.clone, body=%wide.region_2.3_spmd.clone.clone.sunk | while | flops 38273032 | bytes 5538319 | solution.py:65
  32.3 0.6 dynamic_slice.31
  33.4 2.7 %fusion.68 = f32[16,512,64]{1,2,0:T(8,128)} fusion(f32[16,512,64]{1,2,0:T(8,128)} %get-tuple-element.244, s32[]{:T(128)S(6)} %copy.59, f32[512,512]{1,0:T(8,128)} %get-tuple-element.262, s32[512,512]{1,0:T(8,128)S(1)} %reshape.207, f32[512]{0:T(512)S(1)} %bitcast.97, f32[512]{0:T(512)S(1)} %bitcast.95, f32[512]{0:T(512)S(1)} %bitcast.96, ...), kind=kOutput, calls=%fused_computation.3.clone.1 | convolution fusion | flops 38273024 | bytes 2371592 | tf_op jit(solution)/shard_map/while/body/eval_jaxpr/dot_general | solution.py:63
  36.8 0.6 dynamic_slice.31
  38.0 2.7 %fusion.68 = f32[16,512,64]{1,2,0:T(8,128)} fusion(f32[16,512,64]{1,2,0:T(8,128)} %get-tuple-element.244, s32[]{:T(128)S(6)} %copy.59, f32[512,512]{1,0:T(8,128)} %get-tuple-element.262, s32[512,512]{1,0:T(8,128)S(1)} %reshape.207, f32[512]{0:T(512)S(1)} %bitcast.97, f32[512]{0:T(512)S(1)} %bitcast.95, f32[512]{0:T(512)S(1)} %bitcast.96, ...), kind=kOutput, calls=%fused_computation.3.clone.1 | convolution fusion | flops 38273024 | bytes 2371592 | tf_op jit(solution)/shard_map/while/body/eval_jaxpr/dot_general | solution.py:63
  41.5 0.6 dynamic_slice.31
  42.7 2.7 %fusion.68 = f32[16,512,64]{1,2,0:T(8,128)} fusion(f32[16,512,64]{1,2,0:T(8,128)} %get-tuple-element.244, s32[]{:T(128)S(6)} %copy.59, f32[512,512]{1,0:T(8,128)} %get-tuple-element.262, s32[512,512]{1,0:T(8,128)S(1)} %reshape.207, f32[512]{0:T(512)S(1)} %bitcast.97, f32[512]{0:T(512)S(1)} %bitcast.95, f32[512]{0:T(512)S(1)} %bitcast.96, ...), kind=kOutput, calls=%fused_computation.3.clone.1 | convolution fusion | flops 38273024 | bytes 2371592 | tf_op jit(solution)/shard_map/while/body/eval_jaxpr/dot_general | solution.py:63
  46.1 0.6 dynamic_slice.31
  47.2 2.7 %fusion.68 = f32[16,512,64]{1,2,0:T(8,128)} fusion(f32[16,512,64]{1,2,0:T(8,128)} %get-tuple-element.244, s32[]{:T(128)S(6)} %copy.59, f32[512,512]{1,0:T(8,128)} %get-tuple-element.262, s32[512,512]{1,0:T(8,128)S(1)} %reshape.207, f32[512]{0:T(512)S(1)} %bitcast.97, f32[512]{0:T(512)S(1)} %bitcast.95, f32[512]{0:T(512)S(1)} %bitcast.96, ...), kind=kOutput, calls=%fused_computation.3.clone.1 | convolution fusion | flops 38273024 | bytes 2371592 | tf_op jit(solution)/shard_map/while/body/eval_jaxpr/dot_general | solution.py:63
  50.7 0.6 dynamic_slice.31
  51.8 2.7 %fusion.68 = f32[16,512,64]{1,2,0:T(8,128)} fusion(f32[16,512,64]{1,2,0:T(8,128)} %get-tuple-element.244, s32[]{:T(128)S(6)} %copy.59, f32[512,512]{1,0:T(8,128)} %get-tuple-element.262, s32[512,512]{1,0:T(8,128)S(1)} %reshape.207, f32[512]{0:T(512)S(1)} %bitcast.97, f32[512]{0:T(512)S(1)} %bitcast.95, f32[512]{0:T(512)S(1)} %bitcast.96, ...), kind=kOutput, calls=%fused_computation.3.clone.1 | convolution fusion | flops 38273024 | bytes 2371592 | tf_op jit(solution)/shard_map/while/body/eval_jaxpr/dot_general | solution.py:63
  55.2 0.6 dynamic_slice.31
  56.4 2.7 %fusion.68 = f32[16,512,64]{1,2,0:T(8,128)} fusion(f32[16,512,64]{1,2,0:T(8,128)} %get-tuple-element.244, s32[]{:T(128)S(6)} %copy.59, f32[512,512]{1,0:T(8,128)} %get-tuple-element.262, s32[512,512]{1,0:T(8,128)S(1)} %reshape.207, f32[512]{0:T(512)S(1)} %bitcast.97, f32[512]{0:T(512)S(1)} %bitcast.95, f32[512]{0:T(512)S(1)} %bitcast.96, ...), kind=kOutput, calls=%fused_computation.3.clone.1 | convolution fusion | flops 38273024 | bytes 2371592 | tf_op jit(solution)/shard_map/while/body/eval_jaxpr/dot_general | solution.py:63
  59.8 0.6 dynamic_slice.31
  61.0 2.7 %fusion.68 = f32[16,512,64]{1,2,0:T(8,128)} fusion(f32[16,512,64]{1,2,0:T(8,128)} %get-tuple-element.244, s32[]{:T(128)S(6)} %copy.59, f32[512,512]{1,0:T(8,128)} %get-tuple-element.262, s32[512,512]{1,0:T(8,128)S(1)} %reshape.207, f32[512]{0:T(512)S(1)} %bitcast.97, f32[512]{0:T(512)S(1)} %bitcast.95, f32[512]{0:T(512)S(1)} %bitcast.96, ...), kind=kOutput, calls=%fused_computation.3.clone.1 | convolution fusion | flops 38273024 | bytes 2371592 | tf_op jit(solution)/shard_map/while/body/eval_jaxpr/dot_general | solution.py:63
  64.4 0.6 dynamic_slice.31
  65.6 2.7 %fusion.68 = f32[16,512,64]{1,2,0:T(8,128)} fusion(f32[16,512,64]{1,2,0:T(8,128)} %get-tuple-element.244, s32[]{:T(128)S(6)} %copy.59, f32[512,512]{1,0:T(8,128)} %get-tuple-element.262, s32[512,512]{1,0:T(8,128)S(1)} %reshape.207, f32[512]{0:T(512)S(1)} %bitcast.97, f32[512]{0:T(512)S(1)} %bitcast.95, f32[512]{0:T(512)S(1)} %bitcast.96, ...), kind=kOutput, calls=%fused_computation.3.clone.1 | convolution fusion | flops 38273024 | bytes 2371592 | tf_op jit(solution)/shard_map/while/body/eval_jaxpr/dot_general | solution.py:63
  69.0 0.6 dynamic_slice.31
  70.2 2.7 %fusion.68 = f32[16,512,64]{1,2,0:T(8,128)} fusion(f32[16,512,64]{1,2,0:T(8,128)} %get-tuple-element.244, s32[]{:T(128)S(6)} %copy.59, f32[512,512]{1,0:T(8,128)} %get-tuple-element.262, s32[512,512]{1,0:T(8,128)S(1)} %reshape.207, f32[512]{0:T(512)S(1)} %bitcast.97, f32[512]{0:T(512)S(1)} %bitcast.95, f32[512]{0:T(512)S(1)} %bitcast.96, ...), kind=kOutput, calls=%fused_computation.3.clone.1 | convolution fusion | flops 38273024 | bytes 2371592 | tf_op jit(solution)/shard_map/while/body/eval_jaxpr/dot_general | solution.py:63
  73.6 0.6 dynamic_slice.31
  74.7 2.7 %fusion.68 = f32[16,512,64]{1,2,0:T(8,128)} fusion(f32[16,512,64]{1,2,0:T(8,128)} %get-tuple-element.244, s32[]{:T(128)S(6)} %copy.59, f32[512,512]{1,0:T(8,128)} %get-tuple-element.262, s32[512,512]{1,0:T(8,128)S(1)} %reshape.207, f32[512]{0:T(512)S(1)} %bitcast.97, f32[512]{0:T(512)S(1)} %bitcast.95, f32[512]{0:T(512)S(1)} %bitcast.96, ...), kind=kOutput, calls=%fused_computation.3.clone.1 | convolution fusion | flops 38273024 | bytes 2371592 | tf_op jit(solution)/shard_map/while/body/eval_jaxpr/dot_general | solution.py:63
  78.1 0.6 dynamic_slice.31
  79.3 2.7 %fusion.68 = f32[16,512,64]{1,2,0:T(8,128)} fusion(f32[16,512,64]{1,2,0:T(8,128)} %get-tuple-element.244, s32[]{:T(128)S(6)} %copy.59, f32[512,512]{1,0:T(8,128)} %get-tuple-element.262, s32[512,512]{1,0:T(8,128)S(1)} %reshape.207, f32[512]{0:T(512)S(1)} %bitcast.97, f32[512]{0:T(512)S(1)} %bitcast.95, f32[512]{0:T(512)S(1)} %bitcast.96, ...), kind=kOutput, calls=%fused_computation.3.clone.1 | convolution fusion | flops 38273024 | bytes 2371592 | tf_op jit(solution)/shard_map/while/body/eval_jaxpr/dot_general | solution.py:63
  82.7 0.6 dynamic_slice.31
  83.9 2.7 %fusion.68 = f32[16,512,64]{1,2,0:T(8,128)} fusion(f32[16,512,64]{1,2,0:T(8,128)} %get-tuple-element.244, s32[]{:T(128)S(6)} %copy.59, f32[512,512]{1,0:T(8,128)} %get-tuple-element.262, s32[512,512]{1,0:T(8,128)S(1)} %reshape.207, f32[512]{0:T(512)S(1)} %bitcast.97, f32[512]{0:T(512)S(1)} %bitcast.95, f32[512]{0:T(512)S(1)} %bitcast.96, ...), kind=kOutput, calls=%fused_computation.3.clone.1 | convolution fusion | flops 38273024 | bytes 2371592 | tf_op jit(solution)/shard_map/while/body/eval_jaxpr/dot_general | solution.py:63
  87.3 0.6 dynamic_slice.31
  88.5 2.7 %fusion.68 = f32[16,512,64]{1,2,0:T(8,128)} fusion(f32[16,512,64]{1,2,0:T(8,128)} %get-tuple-element.244, s32[]{:T(128)S(6)} %copy.59, f32[512,512]{1,0:T(8,128)} %get-tuple-element.262, s32[512,512]{1,0:T(8,128)S(1)} %reshape.207, f32[512]{0:T(512)S(1)} %bitcast.97, f32[512]{0:T(512)S(1)} %bitcast.95, f32[512]{0:T(512)S(1)} %bitcast.96, ...), kind=kOutput, calls=%fused_computation.3.clone.1 | convolution fusion | flops 38273024 | bytes 2371592 | tf_op jit(solution)/shard_map/while/body/eval_jaxpr/dot_general | solution.py:63
  91.9 0.6 dynamic_slice.31
  93.0 2.7 %fusion.68 = f32[16,512,64]{1,2,0:T(8,128)} fusion(f32[16,512,64]{1,2,0:T(8,128)} %get-tuple-element.244, s32[]{:T(128)S(6)} %copy.59, f32[512,512]{1,0:T(8,128)} %get-tuple-element.262, s32[512,512]{1,0:T(8,128)S(1)} %reshape.207, f32[512]{0:T(512)S(1)} %bitcast.97, f32[512]{0:T(512)S(1)} %bitcast.95, f32[512]{0:T(512)S(1)} %bitcast.96, ...), kind=kOutput, calls=%fused_computation.3.clone.1 | convolution fusion | flops 38273024 | bytes 2371592 | tf_op jit(solution)/shard_map/while/body/eval_jaxpr/dot_general | solution.py:63
  96.5 0.6 dynamic_slice.31
  97.6 2.7 %fusion.68 = f32[16,512,64]{1,2,0:T(8,128)} fusion(f32[16,512,64]{1,2,0:T(8,128)} %get-tuple-element.244, s32[]{:T(128)S(6)} %copy.59, f32[512,512]{1,0:T(8,128)} %get-tuple-element.262, s32[512,512]{1,0:T(8,128)S(1)} %reshape.207, f32[512]{0:T(512)S(1)} %bitcast.97, f32[512]{0:T(512)S(1)} %bitcast.95, f32[512]{0:T(512)S(1)} %bitcast.96, ...), kind=kOutput, calls=%fused_computation.3.clone.1 | convolution fusion | flops 38273024 | bytes 2371592 | tf_op jit(solution)/shard_map/while/body/eval_jaxpr/dot_general | solution.py:63
  101.0 0.6 dynamic_slice.31
  102.2 2.7 %fusion.68 = f32[16,512,64]{1,2,0:T(8,128)} fusion(f32[16,512,64]{1,2,0:T(8,128)} %get-tuple-element.244, s32[]{:T(128)S(6)} %copy.59, f32[512,512]{1,0:T(8,128)} %get-tuple-element.262, s32[512,512]{1,0:T(8,128)S(1)} %reshape.207, f32[512]{0:T(512)S(1)} %bitcast.97, f32[512]{0:T(512)S(1)} %bitcast.95, f32[512]{0:T(512)S(1)} %bitcast.96, ...), kind=kOutput, calls=%fused_computation.3.clone.1 | convolution fusion | flops 38273024 | bytes 2371592 | tf_op jit(solution)/shard_map/while/body/eval_jaxpr/dot_general | solution.py:63
  104.9 1.3 %fusion.57 = (f32[1,16,512]{2,0,1:T(1,128)S(1)}, f32[1,16,512]{2,0,1:T(1,128)S(1)}, f32[1,16,512]{2,0,1:T(1,128)S(1)}) fusion(f32[12,16,512]{2,0,1:T(8,128)} %copy-done.4), kind=kLoop, calls=%fused_computation.88 | loop fusion | bytes 196608 | tf_op jit(solution)/shard_map/slice | solution.py:108
  106.5 6.6 %fusion.32 = f32[2,16,128,64]{2,0,3,1:T(2,128)S(1)} fusion(f32[4,16,128,64]{2,3,1,0:T(8,128)} %bitcast.90, f32[4,16]{0,1:T(8,128)S(1)} %copy.30, f32[4,2]{0,1:T(2,128)S(1)} %compare_convert_fusion), kind=kOutput, calls=%fused_computation.40 | convolution fusion | flops 12583040 | bytes 3146016 | tf_op jit(solution)/shard_map/mh,mj,mhnp->jhnp/dot_general | solution.py:155
  113.1 1.1 fusion.56
  114.2 1.0 fusion.40
  115.2 1.0 fusion.42
  116.2 1.7 %multiply_reduce_fusion = (f32[16,512]{1,0:T(8,128)S(1)}, f32[16,512,64]{1,2,0:T(8,128)S(1)}) fusion(f32[16,512,64]{1,2,0:T(8,128)S(1)} %copy-done.3, f32[16,64,512]{2,1,0:T(8,128)S(1)} %fusion.40, f32[16,512]{1,0:T(8,128)S(1)} %get-tuple-element.169, f32[16,64,512]{2,1,0:T(8,128)S(1)} %fusion.42, f32[16,512]{1,0:T(8,128)S(1)} %get-tuple-element.170, ...), kind=kOutput, calls=%fused_computation.39 | convolution fusion | flops 810147840 | bytes 9207812 | tf_op jit(solution)/shard_map/tn,hnp->htp/dot_general | solution.py:107
  118.4 1.3 %copy.32 = bf16[512,1024]{1,0:T(8,128)(2,1)} copy(bf16[512,1024]{0,1:T(8,128)(2,1)S(1)} %bitcast.88) | data formatting | bytes 2097152 | tf_op jit(solution)/shard_map/convert_element_type | solution.py:115
  (117 shorter events, 14.6 us)
Async XLA Ops:
  6.5 8.7 %copy-start = (bf16[512,128]{1,0:T(8,128)(2,1)S(1)}, bf16[512,128]{1,0:T(8,128)(2,1)}, u32[]{:S(2)}) copy-start(bf16[512,128]{1,0:T(8,128)(2,1)} %param.14) | copy-start | bytes 393220
  6.5 7.1 %copy-start.5 = (bf16[512,128]{1,0:T(8,128)(2,1)S(1)}, bf16[512,128]{1,0:T(8,128)(2,1)}, u32[]{:S(2)}) copy-start(bf16[512,128]{1,0:T(8,128)(2,1)} %param.13) | copy-start | bytes 393220
  6.5 7.6 %copy-start.6 = (s32[12,16,512]{2,1,0:T(8,128)S(1)}, s32[12,16,512]{2,1,0:T(8,128)}, u32[]{:S(2)}) copy-start(s32[12,16,512]{2,1,0:T(8,128)} %param.16) | copy-start | bytes 1179652
  6.5 100.0 %all-gather.4.cloned.1.call-start = ((), (), s32[]{:S(2)}) async-start(), calls=%async_computation | async-start | bytes 2621440 | tf_op jit(solution)/shard_map/all_gather | solution.py:151
  9.0 8.7 %collective-permute-start.1 = (f32[16]{0:T(128)S(1)}, f32[16]{0:T(128)S(1)}, u32[]{:S(2)}, u32[]{:S(2)}) collective-permute-start(f32[16]{0:T(128)S(1)} %slice_reduce_fusion.1), channel_id=1, source_target_pairs={{0,2},{2,0},{1,3},{3,1},{4,6},{6,4},{5,7},{7,5},{8,10},{10,8},{9,1... | collective-permute-start | bytes 200 | tf_op jit(solution)/shard_map/ppermute | solution.py:19
  13.6 2.9 %copy-start.8 = (u32[32]{0:T(128)S(1)}, u32[32]{0:T(128)}, u32[]{:S(2)}) copy-start(u32[32]{0:T(128)} %constant.124) | copy-start | bytes 388
  14.1 16.3 %collective-permute-start = (f32[16,128,64]{1,2,0:T(8,128)S(1)}, f32[16,128,64]{1,2,0:T(8,128)S(1)}, u32[]{:S(2)}, u32[]{:S(2)}) collective-permute-start(f32[16,128,64]{1,2,0:T(8,128)S(1)} %convolution_bitcast_fusion.1), channel_id=1, source_target_pairs={{0,2},{2,0},{1,3},{3,1},{4,6},{6,4},{5,7},{7,5},{8,10},{10,8},{9,1... | collective-permute-start | bytes 1572872 | tf_op jit(solution)/shard_map/ppermute | solution.py:19
  14.5 0.8 copy-start.4
  30.4 1.1 copy-start.1
  31.5 74.7 %copy-start.7 = (f32[1024]{0:T(1024)S(1)}, f32[1024]{0:T(1024)}, u32[]{:S(2)}) copy-start(f32[1024]{0:T(1024)} %param.17) | copy-start | bytes 12292
  114.2 2.0 %copy-start.2 = (f32[16,128,64]{1,2,0:T(8,128)S(1)}, f32[16,128,64]{1,2,0:T(8,128)}, u32[]{:S(2)}) copy-start(f32[16,128,64]{1,2,0:T(8,128)} %copy-done.1) | copy-start | bytes 1572868
  114.2 2.0 %copy-start.3 = (f32[16,512,64]{1,2,0:T(8,128)S(1)}, f32[16,512,64]{1,2,0:T(8,128)}, u32[]{:S(2)}) copy-start(f32[16,512,64]{1,2,0:T(8,128)} %get-tuple-element.88) | copy-start | bytes 6291460
Sparse Core Ops, SparseCore 0:
  31.6 43.8 all-gather.3
where the time goes:
time: 127 us
  matrix products  54.7 us (43%)
  local copies, waits for them, and re-layouts  28.2 us (22%)
  between operations  14.2 us (11%)
  blocking collectives  12.4 us (10%)
  loops' own time  9.64 us (8%)
  other arithmetic  4.24 us (3%)
  starting transfers between devices  3.12 us (2%)
    dot_general x16, matrix products, one_head(): return jnp.dot(mixing, columns, preferred_element_type=jnp.float32)  42.7 us
    unnamed x1, blocking collectives  12.4 us
    dynamic_slice x32, local copies, waits for them, and re-layouts, near_terms(): lax.map(one_head, (cumulative, head_weights, jnp.arange(head_count, dtype...  9.67 us
    another operation x1, loops' own time, near_terms(): lax.map(one_head, (cumulative, head_weights, jnp.arange(head_count, dtype...  9.64 us
    reshape x16, local copies, waits for them, and re-layouts, near_terms(): levels_full = jnp.broadcast_to(levels[:, None, :, None], (block_rows // B...  7.83 us
    dot_general x1, matrix products, local(): jnp.einsum('mh,mj,mhnp->jhnp', coefficient, onehot, shard_piece, precisio...  6.57 us
    dot_general x3, matrix products, finish(): jnp.einsum('tn,hnp->htp', queries, far_levels[slot], precision=highest)  3.71 us
    broadcast_in_dim x16, local copies, waits for them, and re-layouts, near_terms(): jnp.broadcast_to(levels[:, None, :, None], (block_rows // BUCKET, BUCKET,...  3.19 us
  transfers between devices with their start and end apart: 3, of which 0 were waited for; matrix products, arithmetic and copies ran while one was open for 55% of the time, Pallas kernels for 0%

commit v1 on v0

v1 whole, which is shorter than its diff:
```python
import functools

import jax
import jax.numpy as jnp
from jax import lax
from jax.experimental import pallas as pl
from jax.experimental.pallas import tpu as pltpu
from jax.sharding import PartitionSpec as P

BUCKET = 64
LANES = 128
CHUNKS = 4

decay_unit = 1.0 / 65536.0
weight_unit = 1.0 / 256.0
norm_epsilon = 1e-05
masked_out = -1e30

bf16 = jnp.bfloat16
f32 = jnp.float32


def contract_last(a, b):
    return lax.dot_general(a, b, (((1,), (1,)), ((), ())), preferred_element_type=f32)


def split_two(x):
    high = x.astype(bf16)
    return high, (x - high.astype(f32)).astype(bf16)


def decay_exponents(codes):
    heads, tokens = codes.shape
    blocks = tokens // LANES
    high = (codes >> 8).astype(f32).astype(bf16)
    low = (codes & 255).astype(f32).astype(bf16)
    stacked = jnp.concatenate(
        [part[:, LANES * j : LANES * (j + 1)] for j in range(blocks) for part in (high, low)], axis=0
    )
    row = lax.broadcasted_iota(jnp.int32, (LANES, LANES), 0)
    col = lax.broadcasted_iota(jnp.int32, (LANES, LANES), 1)
    same = (row // BUCKET) == (col // BUCKET)
    upto = row <= col

    def sums(mask):
        weights = jnp.where(mask, 1.0, 0.0).astype(bf16)
        out = jnp.dot(stacked, weights, preferred_element_type=f32)
        return [
            out[2 * heads * j : 2 * heads * j + heads] * 256.0
            + out[2 * heads * j + heads : 2 * heads * (j + 1)]
            for j in range(blocks)
        ]

    prefix = {BUCKET: sums(same & upto), LANES: sums(upto)}
    suffix = {BUCKET: sums(same & ~upto), LANES: sums(~upto)}
    total = sums(row >= 0)
    size = 2 * LANES
    while size <= tokens:
        span = size // LANES
        prefix[size], suffix[size] = [], []
        for j in range(blocks):
            start = j // span * span
            prefix[size].append(sum(total[start:j], prefix[LANES][j]))
            suffix[size].append(sum(total[j + 1 : start + span], suffix[LANES][j]))
        size *= 2
    everything = sum(total[1:], total[0])
    join = lambda pieces: jnp.concatenate(pieces, axis=1)
    return (
        {k: join(v) for k, v in prefix.items()},
        {k: join(v) for k, v in suffix.items()},
        everything,
    )


def state_kernel(rows, values_ref, keys_ref, codes_ref, weights_ref, *outs):
    payloads, turned_ref, source_ref, reader_ref, cum_ref = outs[:-4], *outs[-4:]
    heads, tokens = codes_ref.shape
    head_size = values_ref.shape[1] // heads
    prefix, suffix, total = decay_exponents(codes_ref[...])
    cum_ref[...] = prefix[tokens] * -decay_unit
    sizes = [BUCKET]
    while sizes[-1] * 2 < tokens:
        sizes.append(sizes[-1] * 2)
    for i, size in enumerate(sizes):
        source_ref[i] = jnp.exp(suffix[size] * -decay_unit)
    lam = lambda level: weights_ref[level].astype(f32) * weight_unit
    reader_ref[0] = lam(0) * jnp.exp(suffix[BUCKET] * decay_unit)
    for i, size in enumerate(sizes):
        reader_ref[i + 1] = lam(i + 1) * jnp.exp(prefix[size] * -decay_unit)
    to_end = jnp.exp(suffix[tokens] * -decay_unit)
    total = total * -decay_unit
    keys = keys_ref[...]
    chunk_heads = rows // head_size
    for c, payload in enumerate(payloads):
        turned = values_ref[:, rows * c : rows * (c + 1)].T
        turned_ref[rows * c : rows * (c + 1), :] = turned
        decayed = jnp.concatenate(
            [
                (
                    turned[head_size * i : head_size * (i + 1)].astype(f32)
                    * to_end[chunk_heads * c + i : chunk_heads * c + i + 1]
                ).astype(bf16)
                for i in range(chunk_heads)
            ],
            axis=0,
        )
        payload[:rows, :] = jnp.dot(decayed, keys, preferred_element_type=f32)
        payload[rows : rows + chunk_heads, :] = total[chunk_heads * c : chunk_heads * (c + 1)]
        pad = payload.shape[0] - rows - chunk_heads
        if pad:
            payload[rows + chunk_heads :, :] = jnp.zeros((pad, LANES), f32)


def near_kernel(chunk_heads, turned_ref, queries_ref, keys_ref, source_ref, reader_ref, *refs):
    outs, table_ref = refs[:-1], refs[-1]
    tokens = queries_ref.shape[0]
    heads = source_ref.shape[1]
    rows = outs[0].shape[0]
    head_size = rows // chunk_heads
    blocks = tokens // LANES
    row = lax.broadcasted_iota(jnp.int32, (LANES, LANES), 0)
    col = lax.broadcasted_iota(jnp.int32, (LANES, LANES), 1)
    same = (row // BUCKET) == (col // BUCKET)
    for j in range(blocks):
        span = pl.ds(LANES * j, LANES)
        scores = contract_last(keys_ref[span, :], queries_ref[span, :])
        inner = jnp.where(same & (row <= col), scores, 0.0)
        across = jnp.where(~same & (row < col), scores, 0.0)
        table_ref[j] = jnp.concatenate(split_two(jnp.concatenate([inner, across], axis=1)), axis=0)
    wide = {}
    size = LANES
    while size < tokens:
        wide[size] = []
        for start in range(0, tokens, 2 * size):
            scores = contract_last(
                keys_ref[pl.ds(start, size), :], queries_ref[pl.ds(start + size, size), :]
            )
            wide[size].append(jnp.concatenate(split_two(scores), axis=0))
        size *= 2

    def scaled(c, level, low, high):
        pieces = []
        for i in range(chunk_heads):
            part = turned_ref[pl.ds(rows * c + head_size * i, head_size), low:high].astype(f32)
            factor = source_ref[level, chunk_heads * c + i : chunk_heads * c + i + 1, low:high]
            pieces.append((part * factor).astype(bf16))
        piece = jnp.concatenate(pieces, axis=0)
        return jnp.concatenate([piece, piece], axis=1)

    def read(c, level, low, high, product):
        pieces = []
        for i in range(chunk_heads):
            factor = reader_ref[level, chunk_heads * c + i : chunk_heads * c + i + 1, low:high]
            pieces.append(product[head_size * i : head_size * (i + 1)] * factor)
        return jnp.concatenate(pieces, axis=0)

    for c, out in enumerate(outs):
        for j in range(blocks):
            low, high = LANES * j, LANES * (j + 1)
            product = jnp.dot(scaled(c, 0, low, high), table_ref[j], preferred_element_type=f32)
            out[:, low:high] = read(c, 0, low, high, product[:, :LANES]) + read(
                c, 1, low, high, product[:, LANES:]
            )
        level = 2
        for size, tables in wide.items():
            for g, table in enumerate(tables):
                start = 2 * size * g
                product = jnp.dot(
                    scaled(c, level - 1, start, start + size), table, preferred_element_type=f32
                )
                low, high = start + size, start + 2 * size
                out[:, low:high] = out[:, low:high] + read(c, level, low, high, product)
            level += 1


def finish_kernel(chunk, chunk_heads, base_level, far_count, *refs):
    near_ref, queries_ref, cum_ref, weights_ref, gain_ref = refs[:5]
    far_refs, gap_refs = refs[5 : 5 + far_count], refs[5 + far_count : 5 + 2 * far_count]
    out_ref = refs[-1]
    rows, tokens = near_ref.shape
    head_size = rows // chunk_heads
    first = chunk_heads * chunk
    cum = cum_ref[first : first + chunk_heads, :]
    queries = queries_ref[...]
    doubled = jnp.concatenate([queries, queries], axis=1)
    combined = [near_ref[head_size * i : head_size * (i + 1), :] for i in range(chunk_heads)]
    for slot in range(far_count):
        product = contract_last(jnp.concatenate(split_two(far_refs[slot][...]), axis=1), doubled)
        gap = jnp.concatenate([gap_refs[slot][...]] * (tokens // LANES), axis=1)
        lam = weights_ref[base_level + 1 + slot, first : first + chunk_heads, :].astype(f32)
        factor = lam * weight_unit * jnp.exp(cum + gap)
        for i in range(chunk_heads):
            combined[i] = combined[i] + factor[i : i + 1] * product[head_size * i : head_size * (i + 1)]
    gain = jnp.broadcast_to(gain_ref[0:1, rows * chunk : rows * (chunk + 1)], (LANES, rows)).T
    pieces = []
    for i in range(chunk_heads):
        y = combined[i]
        inverse = lax.rsqrt(jnp.sum(y * y, axis=0, keepdims=True) * (1.0 / head_size) + norm_epsilon)
        own_gain = jnp.concatenate(
            [gain[head_size * i : head_size * (i + 1)]] * (tokens // LANES), axis=1
        )
        pieces.append((y * inverse * own_gain).astype(bf16))
    out_ref[...] = jnp.concatenate(pieces, axis=0).T


vmem = functools.partial(pl.BlockSpec, memory_space=pltpu.VMEM)
params = pltpu.CompilerParams(vmem_limit_bytes=56 * 1024 * 1024)


def local(values, key_rows, query_rows, decay_codes, weight_codes, norm_gain):
    heads, tokens = decay_codes.shape
    columns = values.shape[1]
    head_size = columns // heads
    chunks = CHUNKS
    rows = columns // chunks
    chunk_heads = heads // chunks
    state_size = key_rows.shape[1]
    near_levels = (tokens // BUCKET).bit_length()
    padded = rows + -(-chunk_heads // 8) * 8
    tok_count, seq_count = lax.axis_size("tok"), lax.axis_size("seq")
    tok_bits, seq_bits = tok_count.bit_length() - 1, seq_count.bit_length() - 1
    tok_index = lax.axis_index("tok")

    *payloads, turned, source, reader, cum = pl.pallas_call(
        functools.partial(state_kernel, rows),
        name="state",
        out_shape=[jax.ShapeDtypeStruct((padded, state_size), f32)] * chunks
        + [
            jax.ShapeDtypeStruct((columns, tokens), bf16),
            jax.ShapeDtypeStruct((near_levels - 1, heads, tokens), f32),
            jax.ShapeDtypeStruct((near_levels, heads, tokens), f32),
            jax.ShapeDtypeStruct((heads, tokens), f32),
        ],
        in_specs=[vmem()] * 4,
        out_specs=[vmem()] * (chunks + 4),
        compiler_params=params,
    )(values, key_rows, decay_codes, weight_codes)

    near = pl.pallas_call(
        functools.partial(near_kernel, chunk_heads),
        name="near",
        out_shape=[jax.ShapeDtypeStruct((rows, tokens), f32)] * chunks,
        in_specs=[vmem()] * 5,
        out_specs=[vmem()] * chunks,
        scratch_shapes=[pltpu.VMEM((tokens // LANES, 2 * LANES, 2 * LANES), bf16)],
        compiler_params=params,
    )(turned, query_rows, key_rows, source, reader)

    def spread(per_head):
        return jnp.broadcast_to(
            per_head[:, None, :], (chunk_heads, head_size, state_size)
        ).reshape(rows, state_size)

    finished = []
    for c in range(chunks):
        aggregate = payloads[c][:rows]
        total = payloads[c][rows : rows + chunk_heads]
        payload = payloads[c]
        prefix = jnp.zeros_like(total)
        far, gaps = [], []
        for place in range(tok_bits):
            if place:
                payload = jnp.concatenate(
                    [aggregate, total, jnp.zeros((padded - rows - chunk_heads, state_size), f32)]
                )
            pairs = [(i, i ^ (1 << place)) for i in range(tok_count)]
            received = lax.ppermute(payload, "tok", pairs)
            partner, partner_total = received[:rows], received[rows : rows + chunk_heads]
            upper = (tok_index >> place) & 1 == 1
            far.append(partner)
            gaps.append(jnp.where(upper, prefix, masked_out))
            decay = jnp.exp(jnp.where(upper, total, partner_total))
            aggregate = jnp.where(
                upper, spread(decay) * partner + aggregate, spread(decay) * aggregate + partner
            )
            prefix = jnp.where(upper, prefix + partner_total, prefix)
            total = total + partner_total
        group_decay = jnp.exp(total)
        for place in range(seq_bits):
            half = 1 << place
            carried = lax.ppermute(
                aggregate, "seq", [(b + half - 1, b + half) for b in range(0, seq_count, 2 * half)]
            )
            for step in range(1, half):
                carried = carried + lax.ppermute(
                    spread(group_decay) * carried,
                    "seq",
                    [(b + half + step - 1, b + half + step) for b in range(0, seq_count, 2 * half)],
                )
            far.append(carried)
            gaps.append(prefix)
            if place + 1 < seq_bits:
                aggregate = aggregate + spread(group_decay) * carried
        finished.append((far, gaps))

    far_count = tok_bits + seq_bits
    gain = norm_gain.reshape(1, columns)
    out = None
    for c, (far, gaps) in enumerate(finished):
        operands = [near[c], query_rows, cum, weight_codes, gain, *far, *gaps]
        in_specs = [vmem()] * len(operands)
        aliases = {}
        if out is not None:
            aliases = {len(operands): 0}
            operands.append(out)
            in_specs.append(pl.BlockSpec(memory_space=pl.ANY))
        out = pl.pallas_call(
            functools.partial(finish_kernel, c, chunk_heads, near_levels - 1, far_count),
            name=f"finish{c}",
            grid=(1,),
            out_shape=jax.ShapeDtypeStruct((tokens, columns), bf16),
            in_specs=in_specs,
            out_specs=pl.BlockSpec((tokens, rows), lambda i, c=c: (0, c)),
            input_output_aliases=aliases,
            compiler_params=params,
        )(*operands)
    return out


def solution(mesh):
    return jax.shard_map(
        local,
        mesh=mesh,
        in_specs=(
            P(("parts", "seq", "tok"), "head"),
            P(("parts", "seq", "tok"), None),
            P(("parts", "seq", "tok"), None),
            P("head", ("parts", "seq", "tok")),
            P(None, "head", ("parts", "seq", "tok")),
            P("head"),
        ),
        out_specs=P(("parts", "seq", "tok"), "head"),
        check_vma=False,
    )
```

time: 127 us -> 57.7 us (0.45)
  the two profiles are of different devices: /device:TPU:0 before, /device:TPU:22 now
where the time goes in v1:
time: 57.7 us; the launch traced here: 57.2 us
  starting transfers between devices  21.7 us (38%)
  Pallas kernels  17.3 us (30%)
  other arithmetic  9.49 us (16%)
  waiting for transfers between devices  5.42 us (9%)
  local copies, waits for them, and re-layouts  3.05 us (5%)
    ppermute x8, starting transfers between devices, local(): lax.ppermute(aggregate, 'seq', [(b + half - 1, b + half) for b in range(0...  12.5 us
    pallas_call x4, Pallas kernels, local(): pl.pallas_call(functools.partial(finish_kernel, c, chunk_heads, near_leve...  10.5 us
    ppermute x4, starting transfers between devices, local(): lax.ppermute(spread(group_decay) * carried, 'seq', [(b + half + step - 1,...  5.19 us
    ppermute x4, starting transfers between devices, local(): received = lax.ppermute(payload, 'tok', pairs)  4.05 us
    pallas_call x1, Pallas kernels, local(): pl.pallas_call(functools.partial(near_kernel, chunk_heads), name='near',...  3.71 us
    select_n x4, other arithmetic, local(): jnp.where(upper, spread(decay) * partner + aggregate, spread(decay) * agg...  3.63 us
    pallas_call x1, Pallas kernels, local(): pl.pallas_call(functools.partial(state_kernel, rows), name='state', out_s...  3.07 us
    exp x4, other arithmetic, local(): group_decay = jnp.exp(total)  3.02 us
  transfers between devices with their start and end apart: 16, of which 5 were waited for; matrix products, arithmetic and copies ran while one was open for 15% of the time, Pallas kernels for 6%

profile of v1, /device:TPU:22, one launch (start us, length us, event | category | flops | bytes accessed | tf_op | source)
XLA Modules:
  0.0 57.2 jit_solution(9299500613328198020)
XLA Ops:
  0.0 3.1 %state.1 = (f32[264,128]{1,0:T(8,128)}, f32[264,128]{1,0:T(8,128)}, f32[264,128]{1,0:T(8,128)}, f32[264,128]{1,0:T(8,128)}, bf16[1024,512]{1,0:T(8,128)(2,1)}, /...) custom-call(bf16[512,1024]{1,0:T(8,128)(2,1)} %values_ref.1, bf16[512,128]{1,0:T(8,128)(2,1)} %keys_ref.3, ...), custom_call_target="tpu_custom_call" | custom-call | tf_op jit(solution)/shard_map/state/pallas_call | solution.py:224
  3.1 0.5 collective-permute-start.12
  3.6 1.5 %collective-permute-start.8 = (f32[264,128]{1,0:T(8,128)}, f32[264,128]{1,0:T(8,128)S(1)}, u32[]{:S(2)}, u32[]{:S(2)}) collective-permute-start(f32[264,128]{1,0:T(8,128)} %get-tuple-element.26), channel_id=1, source_target_pairs={{0,2},{2,0},{1,3},{3,1},{4,6},{6,4},{5,7},{7,5},{8,10},{10,8},{9,1... | collective-permute-start | bytes 405512 | tf_op jit(solution)/shard_map/ppermute | solution.py:267
  5.1 0.5 collective-permute-start.4
  5.6 1.5 %collective-permute-start = (f32[264,128]{1,0:T(8,128)}, f32[264,128]{1,0:T(8,128)S(1)}, u32[]{:S(2)}, u32[]{:S(2)}) collective-permute-start(f32[264,128]{1,0:T(8,128)} %get-tuple-element.22), channel_id=1, source_target_pairs={{0,2},{2,0},{1,3},{3,1},{4,6},{6,4},{5,7},{7,5},{8,10},{10,8},{9,1... | collective-permute-start | bytes 405512 | tf_op jit(solution)/shard_map/ppermute | solution.py:267
  7.1 2.6 %collective-permute-done.12 = f32[264,128]{1,0:T(8,128)S(1)} collective-permute-done((f32[264,128]{1,0:T(8,128)}, f32[264,128]{1,0:T(8,128)S(1)}, u32[]{:S(2)}, u32[]{:S(2)}) %collective-permute-start.12) | collective-permute-done | bytes 135200 | tf_op jit(solution)/shard_map/ppermute | solution.py:267
  9.7 1.2 %add_exponential_fusion = (f32[4,128]{1,0:T(4,128)S(1)}, f32[4,128]{1,0:T(4,128)S(1)}, f32[4,128]{1,0:T(4,128)}) fusion(f32[264,128]{1,0:T(8,128)} %get-tuple-element.28, f32[264,128]{1,0:T(8,128)S(1)} %collective-permute-done.12, pred[]{:T(512)S(6)} %eq.2), kind=kLoop, calls=%fused_computation.32 | loop fusion | flops 1536 | bytes 10241 | tf_op jit(solution)/shard_map/exp | solution.py:278
  11.0 1.6 %fusion.13 = (f32[256,128]{1,0:T(8,128)S(1)}, f32[256,128]{1,0:T(8,128)}) fusion(f32[264,128]{1,0:T(8,128)} %get-tuple-element.28, f32[4,128]{1,0:T(4,128)S(1)} %get-tuple-element.30, pred[]{:T(512)S(6)} %eq.2, f32[264,128]{1,0:T(8,128)S(1)} %collective-permute-done.12), kind=kLoop, calls=%fused_computation.29 | loop fusion | flops 163840 | bytes 526337 | tf_op jit(solution)/shard_map/jit(_where)/select_n | solution.py:273
  12.6 3.5 %collective-permute-start.13 = (f32[256,128]{1,0:T(8,128)S(1)}, f32[256,128]{1,0:T(8,128)S(1)}, u32[]{:S(2)}, u32[]{:S(2)}) collective-permute-start(f32[256,128]{1,0:T(8,128)S(1)} %get-tuple-element.38), channel_id=1, source_target_pairs={{0,4},{8,12},{1,5},{9,13},{2,6},{10,14},{3,7},{11,15},{16,20},{24,... | collective-permute-start | bytes 393224 | tf_op jit(solution)/shard_map/ppermute | solution.py:281
  16.1 0.6 %add_exponential_fusion.1 = (f32[4,128]{1,0:T(4,128)S(1)}, f32[4,128]{1,0:T(4,128)S(1)}, f32[4,128]{1,0:T(4,128)}) fusion(f32[264,128]{1,0:T(8,128)S(1)} %copy-done.6, f32[264,128]{1,0:T(8,128)S(1)} %collective-permute-done.8, pred[]{:T(512)S(6)} %eq.2), kind=kLoop, calls=%fused_computation.34 | loop fusion | flops 1536 | bytes 10241 | tf_op jit(solution)/shard_map/exp | solution.py:278
  16.7 0.7 %fusion.9 = (f32[256,128]{1,0:T(8,128)S(1)}, f32[256,128]{1,0:T(8,128)}) fusion(f32[264,128]{1,0:T(8,128)S(1)} %copy-done.6, f32[4,128]{1,0:T(4,128)S(1)} %get-tuple-element.32, pred[]{:T(512)S(6)} %eq.2, f32[264,128]{1,0:T(8,128)S(1)} %collective-permute-done.8), kind=kLoop, calls=%fused_computation.25 | loop fusion | flops 163840 | bytes 526337 | tf_op jit(solution)/shard_map/jit(_where)/select_n | solution.py:273
  17.4 1.3 %collective-permute-start.9 = (f32[256,128]{1,0:T(8,128)S(1)}, f32[256,128]{1,0:T(8,128)S(1)}, u32[]{:S(2)}, u32[]{:S(2)}) collective-permute-start(f32[256,128]{1,0:T(8,128)S(1)} %get-tuple-element.41), channel_id=1, source_target_pairs={{0,4},{8,12},{1,5},{9,13},{2,6},{10,14},{3,7},{11,15},{16,20},{24,... | collective-permute-start | bytes 393224 | tf_op jit(solution)/shard_map/ppermute | solution.py:281
  18.7 0.0 collective-permute-done.4
  18.7 0.6 %add_exponential_fusion.2 = (f32[4,128]{1,0:T(4,128)S(1)}, f32[4,128]{1,0:T(4,128)S(1)}, f32[4,128]{1,0:T(4,128)}) fusion(f32[264,128]{1,0:T(8,128)S(1)} %copy-done.5, f32[264,128]{1,0:T(8,128)S(1)} %collective-permute-done.4, pred[]{:T(512)S(6)} %eq.2), kind=kLoop, calls=%fused_computation.36 | loop fusion | flops 1536 | bytes 10241 | tf_op jit(solution)/shard_map/exp | solution.py:278
  19.3 0.7 %fusion.5 = (f32[256,128]{1,0:T(8,128)S(1)}, f32[256,128]{1,0:T(8,128)}) fusion(f32[264,128]{1,0:T(8,128)S(1)} %copy-done.5, f32[4,128]{1,0:T(4,128)S(1)} %get-tuple-element.34, pred[]{:T(512)S(6)} %eq.2, f32[264,128]{1,0:T(8,128)S(1)} %collective-permute-done.4), kind=kLoop, calls=%fused_computation.21 | loop fusion | flops 163840 | bytes 526337 | tf_op jit(solution)/shard_map/jit(_where)/select_n | solution.py:273
  20.0 1.3 %collective-permute-start.5 = (f32[256,128]{1,0:T(8,128)S(1)}, f32[256,128]{1,0:T(8,128)S(1)}, u32[]{:S(2)}, u32[]{:S(2)}) collective-permute-start(f32[256,128]{1,0:T(8,128)S(1)} %get-tuple-element.44), channel_id=1, source_target_pairs={{0,4},{8,12},{1,5},{9,13},{2,6},{10,14},{3,7},{11,15},{16,20},{24,... | collective-permute-start | bytes 393224 | tf_op jit(solution)/shard_map/ppermute | solution.py:281
  21.2 0.0 collective-permute-done
  21.3 0.6 %add_exponential_fusion.3 = (f32[4,128]{1,0:T(4,128)S(1)}, f32[4,128]{1,0:T(4,128)S(1)}, f32[4,128]{1,0:T(4,128)}) fusion(f32[264,128]{1,0:T(8,128)S(1)} %copy-done.4, f32[264,128]{1,0:T(8,128)S(1)} %collective-permute-done, pred[]{:T(512)S(6)} %eq.2), kind=kLoop, calls=%fused_computation.38 | loop fusion | flops 1536 | bytes 10241 | tf_op jit(solution)/shard_map/exp | solution.py:278
  21.9 0.7 %fusion.1 = (f32[256,128]{1,0:T(8,128)S(1)}, f32[256,128]{1,0:T(8,128)}) fusion(f32[264,128]{1,0:T(8,128)S(1)} %copy-done.4, f32[4,128]{1,0:T(4,128)S(1)} %get-tuple-element.36, pred[]{:T(512)S(6)} %eq.2, f32[264,128]{1,0:T(8,128)S(1)} %collective-permute-done), kind=kLoop, calls=%fused_computation.17 | loop fusion | flops 163840 | bytes 526337 | tf_op jit(solution)/shard_map/jit(_where)/select_n | solution.py:273
  22.5 1.3 %collective-permute-start.1 = (f32[256,128]{1,0:T(8,128)S(1)}, f32[256,128]{1,0:T(8,128)S(1)}, u32[]{:S(2)}, u32[]{:S(2)}) collective-permute-start(f32[256,128]{1,0:T(8,128)S(1)} %get-tuple-element.47), channel_id=1, source_target_pairs={{0,4},{8,12},{1,5},{9,13},{2,6},{10,14},{3,7},{11,15},{16,20},{24,... | collective-permute-start | bytes 393224 | tf_op jit(solution)/shard_map/ppermute | solution.py:281
  23.9 0.6 %copy-done = f32[256,128]{1,0:T(8,128)} copy-done((f32[256,128]{1,0:T(8,128)}, f32[256,128]{1,0:T(8,128)S(1)}, u32[]{:S(2)}) %copy-start) | copy-done | bytes 131096
  24.5 1.3 %collective-permute-start.14 = (f32[256,128]{1,0:T(8,128)S(1)}, f32[256,128]{1,0:T(8,128)S(1)}, u32[]{:S(2)}, u32[]{:S(2)}) collective-permute-start(f32[256,128]{1,0:T(8,128)S(1)} %fusion.15), channel_id=1, source_target_pairs={{4,8},{5,9},{6,10},{7,11},{20,24},{21,25},{22,26},{23,27}} | collective-permute-start | bytes 393224 | tf_op jit(solution)/shard_map/ppermute | solution.py:281
  25.8 0.6 %copy-done.1 = f32[256,128]{1,0:T(8,128)} copy-done((f32[256,128]{1,0:T(8,128)}, f32[256,128]{1,0:T(8,128)S(1)}, u32[]{:S(2)}) %copy-start.1) | copy-done | bytes 131096
  26.4 1.3 %collective-permute-start.10 = (f32[256,128]{1,0:T(8,128)S(1)}, f32[256,128]{1,0:T(8,128)S(1)}, u32[]{:S(2)}, u32[]{:S(2)}) collective-permute-start(f32[256,128]{1,0:T(8,128)S(1)} %fusion.11), channel_id=1, source_target_pairs={{4,8},{5,9},{6,10},{7,11},{20,24},{21,25},{22,26},{23,27}} | collective-permute-start | bytes 393224 | tf_op jit(solution)/shard_map/ppermute | solution.py:281
  27.7 0.0 collective-permute-done.5.refs_6_
  27.8 0.6 %copy-done.2 = f32[256,128]{1,0:T(8,128)} copy-done((f32[256,128]{1,0:T(8,128)}, f32[256,128]{1,0:T(8,128)S(1)}, u32[]{:S(2)}) %copy-start.2) | copy-done | bytes 131096
  28.4 1.3 %collective-permute-start.6 = (f32[256,128]{1,0:T(8,128)S(1)}, f32[256,128]{1,0:T(8,128)S(1)}, u32[]{:S(2)}, u32[]{:S(2)}) collective-permute-start(f32[256,128]{1,0:T(8,128)S(1)} %fusion.7), channel_id=1, source_target_pairs={{4,8},{5,9},{6,10},{7,11},{20,24},{21,25},{22,26},{23,27}} | collective-permute-start | bytes 393224 | tf_op jit(solution)/shard_map/ppermute | solution.py:281
  29.7 0.6 %copy-done.3 = f32[256,128]{1,0:T(8,128)} copy-done((f32[256,128]{1,0:T(8,128)}, f32[256,128]{1,0:T(8,128)S(1)}, u32[]{:S(2)}) %copy-start.3) | copy-done | bytes 131096
  30.3 1.3 %collective-permute-start.2 = (f32[256,128]{1,0:T(8,128)S(1)}, f32[256,128]{1,0:T(8,128)S(1)}, u32[]{:S(2)}, u32[]{:S(2)}) collective-permute-start(f32[256,128]{1,0:T(8,128)S(1)} %fusion.3), channel_id=1, source_target_pairs={{4,8},{5,9},{6,10},{7,11},{20,24},{21,25},{22,26},{23,27}} | collective-permute-start | bytes 393224 | tf_op jit(solution)/shard_map/ppermute | solution.py:281
  31.6 0.6 %collective-permute-done.14 = f32[256,128]{1,0:T(8,128)S(1)} collective-permute-done((f32[256,128]{1,0:T(8,128)S(1)}, f32[256,128]{1,0:T(8,128)S(1)}, u32[]{:S(2)}, u32[]{:S(2)}) %collective-permute-start.14) | collective-permute-done | bytes 131104 | tf_op jit(solution)/shard_map/ppermute | solution.py:281
  32.2 1.3 %collective-permute-start.15 = (f32[256,128]{1,0:T(8,128)S(1)}, f32[256,128]{1,0:T(8,128)S(1)}, u32[]{:S(2)}, u32[]{:S(2)}) collective-permute-start(f32[256,128]{1,0:T(8,128)S(1)} %bitcast_multiply_fusion), channel_id=1, source_target_pairs={{8,12},{9,13},{10,14},{11,15},{24,28},{25,29},{26,30},{27,31}} | collective-permute-start | bytes 393224 | tf_op jit(solution)/shard_map/ppermute | solution.py:285
  33.5 1.5 %collective-permute-done.10 = f32[256,128]{1,0:T(8,128)S(1)} collective-permute-done((f32[256,128]{1,0:T(8,128)S(1)}, f32[256,128]{1,0:T(8,128)S(1)}, u32[]{:S(2)}, u32[]{:S(2)}) %collective-permute-start.10) | collective-permute-done | bytes 131104 | tf_op jit(solution)/shard_map/ppermute | solution.py:281
  35.0 1.3 %collective-permute-start.11 = (f32[256,128]{1,0:T(8,128)S(1)}, f32[256,128]{1,0:T(8,128)S(1)}, u32[]{:S(2)}, u32[]{:S(2)}) collective-permute-start(f32[256,128]{1,0:T(8,128)S(1)} %bitcast_multiply_fusion.4), channel_id=1, source_target_pairs={{8,12},{9,13},{10,14},{11,15},{24,28},{25,29},{26,30},{27,31}} | collective-permute-start | bytes 393224 | tf_op jit(solution)/shard_map/ppermute | solution.py:285
  36.4 0.6 %collective-permute-done.6 = f32[256,128]{1,0:T(8,128)S(1)} collective-permute-done((f32[256,128]{1,0:T(8,128)S(1)}, f32[256,128]{1,0:T(8,128)S(1)}, u32[]{:S(2)}, u32[]{:S(2)}) %collective-permute-start.6) | collective-permute-done | bytes 131104 | tf_op jit(solution)/shard_map/ppermute | solution.py:281
  37.0 1.3 %collective-permute-start.7 = (f32[256,128]{1,0:T(8,128)S(1)}, f32[256,128]{1,0:T(8,128)S(1)}, u32[]{:S(2)}, u32[]{:S(2)}) collective-permute-start(f32[256,128]{1,0:T(8,128)S(1)} %bitcast_multiply_fusion.8), channel_id=1, source_target_pairs={{8,12},{9,13},{10,14},{11,15},{24,28},{25,29},{26,30},{27,31}} | collective-permute-start | bytes 393224 | tf_op jit(solution)/shard_map/ppermute | solution.py:285
  38.3 0.1 collective-permute-done.2
  38.4 1.3 %collective-permute-start.3 = (f32[256,128]{1,0:T(8,128)S(1)}, f32[256,128]{1,0:T(8,128)S(1)}, u32[]{:S(2)}, u32[]{:S(2)}) collective-permute-start(f32[256,128]{1,0:T(8,128)S(1)} %bitcast_multiply_fusion.12), channel_id=1, source_target_pairs={{8,12},{9,13},{10,14},{11,15},{24,28},{25,29},{26,30},{27,31}} | collective-permute-start | bytes 393224 | tf_op jit(solution)/shard_map/ppermute | solution.py:285
  39.7 3.7 %near.1 = (f32[256,512]{1,0:T(8,128)}, f32[256,512]{1,0:T(8,128)}, f32[256,512]{1,0:T(8,128)}, f32[256,512]{1,0:T(8,128)}) custom-call(bf16[1024,512]{1,0:T(8,128)(2,1)} %get-tuple-element.17.turned_ref, bf16[512,128]{1,0:T(8,128)(2,1)} %refs_1_.7, bf16[512,128]{1,0:T(8,128)(2,1)} %keys_ref.3, f32[3,16,512]{2,1,0:T(8,128)} %get-tuple-element.18.source_ref, ...), custom_call_target="tpu_custom_call" | custom-call | tf_op jit(solution)/shard_map/near/pallas_call | solution.py:239
  43.4 0.0 collective-permute-done.15
  43.4 0.7 %add.79.refs_7_ = f32[256,128]{1,0:T(8,128)} add(f32[256,128]{1,0:T(8,128)S(1)} %collective-permute-done.14, f32[256,128]{1,0:T(8,128)S(1)} %collective-permute-done.15) | non-fusion elementwise | flops 32768 | bytes 393216 | tf_op jit(solution)/shard_map/add | solution.py:285
  44.1 0.7 %add.74.refs_7_ = f32[256,128]{1,0:T(8,128)} add(f32[256,128]{1,0:T(8,128)S(1)} %collective-permute-done.10, f32[256,128]{1,0:T(8,128)S(1)} %collective-permute-done.11) | non-fusion elementwise | flops 32768 | bytes 393216 | tf_op jit(solution)/shard_map/add | solution.py:285
  44.7 0.7 %add.69.refs_7_ = f32[256,128]{1,0:T(8,128)} add(f32[256,128]{1,0:T(8,128)S(1)} %collective-permute-done.6, f32[256,128]{1,0:T(8,128)S(1)} %collective-permute-done.7) | non-fusion elementwise | flops 32768 | bytes 393216 | tf_op jit(solution)/shard_map/add | solution.py:285
  45.4 0.7 %add.64.refs_7_ = f32[256,128]{1,0:T(8,128)} add(f32[256,128]{1,0:T(8,128)S(1)} %collective-permute-done.2, f32[256,128]{1,0:T(8,128)S(1)} %collective-permute-done.3) | non-fusion elementwise | flops 32768 | bytes 393216 | tf_op jit(solution)/shard_map/add | solution.py:285
  46.1 0.6 %select_n.75.refs_8_ = f32[4,128]{1,0:T(4,128)} broadcast(f32[]{:T(128)S(6)} %select_n.74), dimensions={} | broadcast | bytes 2052 | tf_op jit(solution)/shard_map/jit(_where)/select_n | solution.py:272
  46.7 2.6 %finish0.1.refs_11_ = bf16[512,1024]{1,0:T(8,128)(2,1)} custom-call(f32[256,512]{1,0:T(8,128)} %get-tuple-element.27.refs_0_, bf16[512,128]{1,0:T(8,128)(2,1)} %refs_1_.7, f32[16,512]{1,0:T(8,128)} %get-tuple-element.21.refs_2_, s32[12,16,512]{2,1,0:T(8,128)} %refs_3_.7, f32[1,1024]{1,0:T(1,128)} %bitcast.65, f32[256,128]{1,0:T(8,128)} %get-tuple-element.39.refs_5_, ...), custom_call_target="tpu_custom_call" | custom-call | tf_op jit(solution)/shard_map/finish0/pallas_call | solution.py:307
  49.3 2.6 %finish1.1.refs_11_ = bf16[512,1024]{1,0:T(8,128)(2,1)} custom-call(f32[256,512]{1,0:T(8,128)} %get-tuple-element.25.refs_0_, bf16[512,128]{1,0:T(8,128)(2,1)} %refs_1_.7, f32[16,512]{1,0:T(8,128)} %get-tuple-element.21.refs_2_, s32[12,16,512]{2,1,0:T(8,128)} %refs_3_.7, f32[1,1024]{1,0:T(1,128)} %bitcast.66, ...), custom_call_target="tpu_custom_call", output_to_operand_aliasing={{}: (11, {})} | custom-call | tf_op jit(solution)/shard_map/finish1/pallas_call | solution.py:307
  51.9 2.6 %finish2.1.refs_11_ = bf16[512,1024]{1,0:T(8,128)(2,1)} custom-call(f32[256,512]{1,0:T(8,128)} %get-tuple-element.23.refs_0_, bf16[512,128]{1,0:T(8,128)(2,1)} %refs_1_.7, f32[16,512]{1,0:T(8,128)} %get-tuple-element.21.refs_2_, s32[12,16,512]{2,1,0:T(8,128)} %refs_3_.7, f32[1,1024]{1,0:T(1,128)} %bitcast.67, ...), custom_call_target="tpu_custom_call", output_to_operand_aliasing={{}: (11, {})} | custom-call | tf_op jit(solution)/shard_map/finish2/pallas_call | solution.py:307
  54.6 2.6 %finish3.1 = bf16[512,1024]{1,0:T(8,128)(2,1)} custom-call(f32[256,512]{1,0:T(8,128)} %get-tuple-element.20.refs_0_, bf16[512,128]{1,0:T(8,128)(2,1)} %refs_1_.7, f32[16,512]{1,0:T(8,128)} %get-tuple-element.21.refs_2_, s32[12,16,512]{2,1,0:T(8,128)} %refs_3_.7, f32[1,1024]{1,0:T(1,128)} %bitcast.68, ...), custom_call_target="tpu_custom_call", output_to_operand_aliasing={{}: (11, {})} | custom-call | tf_op jit(solution)/shard_map/finish3/pallas_call | solution.py:307
  (25 shorter events, 0.2 us)
Async XLA Ops:
  3.1 6.7 %collective-permute-start.12 = (f32[264,128]{1,0:T(8,128)}, f32[264,128]{1,0:T(8,128)S(1)}, u32[]{:S(2)}, u32[]{:S(2)}) collective-permute-start(f32[264,128]{1,0:T(8,128)} %get-tuple-element.28), channel_id=1, source_target_pairs={{0,2},{2,0},{1,3},{3,1},{4,6},{6,4},{5,7},{7,5},{8,10},{10,8},{9,1... | collective-permute-start | bytes 405512 | tf_op jit(solution)/shard_map/ppermute | solution.py:267
  3.6 12.5 %collective-permute-start.8 = (f32[264,128]{1,0:T(8,128)}, f32[264,128]{1,0:T(8,128)S(1)}, u32[]{:S(2)}, u32[]{:S(2)}) collective-permute-start(f32[264,128]{1,0:T(8,128)} %get-tuple-element.26), channel_id=1, source_target_pairs={{0,2},{2,0},{1,3},{3,1},{4,6},{6,4},{5,7},{7,5},{8,10},{10,8},{9,1... | collective-permute-start | bytes 405512 | tf_op jit(solution)/shard_map/ppermute | solution.py:267
  5.1 13.6 %collective-permute-start.4 = (f32[264,128]{1,0:T(8,128)}, f32[264,128]{1,0:T(8,128)S(1)}, u32[]{:S(2)}, u32[]{:S(2)}) collective-permute-start(f32[264,128]{1,0:T(8,128)} %get-tuple-element.24), channel_id=1, source_target_pairs={{0,2},{2,0},{1,3},{3,1},{4,6},{6,4},{5,7},{7,5},{8,10},{10,8},{9,1... | collective-permute-start | bytes 405512 | tf_op jit(solution)/shard_map/ppermute | solution.py:267
  5.6 15.6 %collective-permute-start = (f32[264,128]{1,0:T(8,128)}, f32[264,128]{1,0:T(8,128)S(1)}, u32[]{:S(2)}, u32[]{:S(2)}) collective-permute-start(f32[264,128]{1,0:T(8,128)} %get-tuple-element.22), channel_id=1, source_target_pairs={{0,2},{2,0},{1,3},{3,1},{4,6},{6,4},{5,7},{7,5},{8,10},{10,8},{9,1... | collective-permute-start | bytes 405512 | tf_op jit(solution)/shard_map/ppermute | solution.py:267
  11.0 5.1 %copy-start.6 = (f32[264,128]{1,0:T(8,128)S(1)}, f32[264,128]{1,0:T(8,128)}, u32[]{:S(2)}) copy-start(f32[264,128]{1,0:T(8,128)} %get-tuple-element.26) | copy-start | bytes 405508
  12.6 11.2 %collective-permute-start.13 = (f32[256,128]{1,0:T(8,128)S(1)}, f32[256,128]{1,0:T(8,128)S(1)}, u32[]{:S(2)}, u32[]{:S(2)}) collective-permute-start(f32[256,128]{1,0:T(8,128)S(1)} %get-tuple-element.38), channel_id=1, source_target_pairs={{0,4},{8,12},{1,5},{9,13},{2,6},{10,14},{3,7},{11,15},{16,20},{24,... | collective-permute-start | bytes 393224 | tf_op jit(solution)/shard_map/ppermute | solution.py:281
  16.7 2.0 %copy-start.5 = (f32[264,128]{1,0:T(8,128)S(1)}, f32[264,128]{1,0:T(8,128)}, u32[]{:S(2)}) copy-start(f32[264,128]{1,0:T(8,128)} %get-tuple-element.24) | copy-start | bytes 405508
  17.4 8.4 %collective-permute-start.9 = (f32[256,128]{1,0:T(8,128)S(1)}, f32[256,128]{1,0:T(8,128)S(1)}, u32[]{:S(2)}, u32[]{:S(2)}) collective-permute-start(f32[256,128]{1,0:T(8,128)S(1)} %get-tuple-element.41), channel_id=1, source_target_pairs={{0,4},{8,12},{1,5},{9,13},{2,6},{10,14},{3,7},{11,15},{16,20},{24,... | collective-permute-start | bytes 393224 | tf_op jit(solution)/shard_map/ppermute | solution.py:281
  19.3 2.0 %copy-start.4 = (f32[264,128]{1,0:T(8,128)S(1)}, f32[264,128]{1,0:T(8,128)}, u32[]{:S(2)}) copy-start(f32[264,128]{1,0:T(8,128)} %get-tuple-element.22) | copy-start | bytes 405508
  20.0 7.8 %collective-permute-start.5 = (f32[256,128]{1,0:T(8,128)S(1)}, f32[256,128]{1,0:T(8,128)S(1)}, u32[]{:S(2)}, u32[]{:S(2)}) collective-permute-start(f32[256,128]{1,0:T(8,128)S(1)} %get-tuple-element.44), channel_id=1, source_target_pairs={{0,4},{8,12},{1,5},{9,13},{2,6},{10,14},{3,7},{11,15},{16,20},{24,... | collective-permute-start | bytes 393224 | tf_op jit(solution)/shard_map/ppermute | solution.py:281
  22.5 7.1 %collective-permute-start.1 = (f32[256,128]{1,0:T(8,128)S(1)}, f32[256,128]{1,0:T(8,128)S(1)}, u32[]{:S(2)}, u32[]{:S(2)}) collective-permute-start(f32[256,128]{1,0:T(8,128)S(1)} %get-tuple-element.47), channel_id=1, source_target_pairs={{0,4},{8,12},{1,5},{9,13},{2,6},{10,14},{3,7},{11,15},{16,20},{24,... | collective-permute-start | bytes 393224 | tf_op jit(solution)/shard_map/ppermute | solution.py:281
  23.8 0.6 %copy-start = (f32[256,128]{1,0:T(8,128)}, f32[256,128]{1,0:T(8,128)S(1)}, u32[]{:S(2)}) copy-start(f32[256,128]{1,0:T(8,128)S(1)} %collective-permute-done.13.refs_6_) | copy-start | bytes 393220
  24.5 7.7 %collective-permute-start.14 = (f32[256,128]{1,0:T(8,128)S(1)}, f32[256,128]{1,0:T(8,128)S(1)}, u32[]{:S(2)}, u32[]{:S(2)}) collective-permute-start(f32[256,128]{1,0:T(8,128)S(1)} %fusion.15), channel_id=1, source_target_pairs={{4,8},{5,9},{6,10},{7,11},{20,24},{21,25},{22,26},{23,27}} | collective-permute-start | bytes 393224 | tf_op jit(solution)/shard_map/ppermute | solution.py:281
  25.8 0.7 %copy-start.1 = (f32[256,128]{1,0:T(8,128)}, f32[256,128]{1,0:T(8,128)S(1)}, u32[]{:S(2)}) copy-start(f32[256,128]{1,0:T(8,128)S(1)} %collective-permute-done.9.refs_6_) | copy-start | bytes 393220
  26.4 8.6 %collective-permute-start.10 = (f32[256,128]{1,0:T(8,128)S(1)}, f32[256,128]{1,0:T(8,128)S(1)}, u32[]{:S(2)}, u32[]{:S(2)}) collective-permute-start(f32[256,128]{1,0:T(8,128)S(1)} %fusion.11), channel_id=1, source_target_pairs={{4,8},{5,9},{6,10},{7,11},{20,24},{21,25},{22,26},{23,27}} | collective-permute-start | bytes 393224 | tf_op jit(solution)/shard_map/ppermute | solution.py:281
  27.7 0.6 %copy-start.2 = (f32[256,128]{1,0:T(8,128)}, f32[256,128]{1,0:T(8,128)S(1)}, u32[]{:S(2)}) copy-start(f32[256,128]{1,0:T(8,128)S(1)} %collective-permute-done.5.refs_6_) | copy-start | bytes 393220
  28.4 8.6 %collective-permute-start.6 = (f32[256,128]{1,0:T(8,128)S(1)}, f32[256,128]{1,0:T(8,128)S(1)}, u32[]{:S(2)}, u32[]{:S(2)}) collective-permute-start(f32[256,128]{1,0:T(8,128)S(1)} %fusion.7), channel_id=1, source_target_pairs={{4,8},{5,9},{6,10},{7,11},{20,24},{21,25},{22,26},{23,27}} | collective-permute-start | bytes 393224 | tf_op jit(solution)/shard_map/ppermute | solution.py:281
  29.7 0.6 %copy-start.3 = (f32[256,128]{1,0:T(8,128)}, f32[256,128]{1,0:T(8,128)S(1)}, u32[]{:S(2)}) copy-start(f32[256,128]{1,0:T(8,128)S(1)} %collective-permute-done.1.refs_6_) | copy-start | bytes 393220
  30.3 8.0 %collective-permute-start.2 = (f32[256,128]{1,0:T(8,128)S(1)}, f32[256,128]{1,0:T(8,128)S(1)}, u32[]{:S(2)}, u32[]{:S(2)}) collective-permute-start(f32[256,128]{1,0:T(8,128)S(1)} %fusion.3), channel_id=1, source_target_pairs={{4,8},{5,9},{6,10},{7,11},{20,24},{21,25},{22,26},{23,27}} | collective-permute-start | bytes 393224 | tf_op jit(solution)/shard_map/ppermute | solution.py:281
  32.2 11.2 %collective-permute-start.15 = (f32[256,128]{1,0:T(8,128)S(1)}, f32[256,128]{1,0:T(8,128)S(1)}, u32[]{:S(2)}, u32[]{:S(2)}) collective-permute-start(f32[256,128]{1,0:T(8,128)S(1)} %bitcast_multiply_fusion), channel_id=1, source_target_pairs={{8,12},{9,13},{10,14},{11,15},{24,28},{25,29},{26,30},{27,31}} | collective-permute-start | bytes 393224 | tf_op jit(solution)/shard_map/ppermute | solution.py:285
  35.0 9.0 %collective-permute-start.11 = (f32[256,128]{1,0:T(8,128)S(1)}, f32[256,128]{1,0:T(8,128)S(1)}, u32[]{:S(2)}, u32[]{:S(2)}) collective-permute-start(f32[256,128]{1,0:T(8,128)S(1)} %bitcast_multiply_fusion.4), channel_id=1, source_target_pairs={{8,12},{9,13},{10,14},{11,15},{24,28},{25,29},{26,30},{27,31}} | collective-permute-start | bytes 393224 | tf_op jit(solution)/shard_map/ppermute | solution.py:285
  37.0 7.8 %collective-permute-start.7 = (f32[256,128]{1,0:T(8,128)S(1)}, f32[256,128]{1,0:T(8,128)S(1)}, u32[]{:S(2)}, u32[]{:S(2)}) collective-permute-start(f32[256,128]{1,0:T(8,128)S(1)} %bitcast_multiply_fusion.8), channel_id=1, source_target_pairs={{8,12},{9,13},{10,14},{11,15},{24,28},{25,29},{26,30},{27,31}} | collective-permute-start | bytes 393224 | tf_op jit(solution)/shard_map/ppermute | solution.py:285
  38.4 7.0 %collective-permute-start.3 = (f32[256,128]{1,0:T(8,128)S(1)}, f32[256,128]{1,0:T(8,128)S(1)}, u32[]{:S(2)}, u32[]{:S(2)}) collective-permute-start(f32[256,128]{1,0:T(8,128)S(1)} %bitcast_multiply_fusion.12), channel_id=1, source_target_pairs={{8,12},{9,13},{10,14},{11,15},{24,28},{25,29},{26,30},{27,31}} | collective-permute-start | bytes 393224 | tf_op jit(solution)/shard_map/ppermute | solution.py:285

commit v2 on v1

v2 whole, which is shorter than its diff:
```python
import functools

import jax
import jax.numpy as jnp
from jax import lax
from jax.experimental import pallas as pl
from jax.experimental.pallas import tpu as pltpu
from jax.sharding import PartitionSpec as P


BUCKET = 64
LANES = 128
PIECES = 2

decay_unit = 1.0 / 65536.0
weight_unit = 1.0 / 256.0
norm_epsilon = 1e-05
masked_out = -1e30

bf16 = jnp.bfloat16
f32 = jnp.float32


def contract_last(a, b):
    return lax.dot_general(a, b, (((1,), (1,)), ((), ())), preferred_element_type=f32)


def split_two(x):
    high = x.astype(bf16)
    return high, (x - high.astype(f32)).astype(bf16)


def decay_exponents(codes):
    heads, tokens = codes.shape
    blocks = tokens // LANES
    high = (codes >> 8).astype(f32).astype(bf16)
    low = (codes & 255).astype(f32).astype(bf16)
    stacked = jnp.concatenate(
        [part[:, LANES * j : LANES * (j + 1)] for j in range(blocks) for part in (high, low)], axis=0
    )
    row = lax.broadcasted_iota(jnp.int32, (LANES, LANES), 0)
    col = lax.broadcasted_iota(jnp.int32, (LANES, LANES), 1)
    same = (row // BUCKET) == (col // BUCKET)
    upto = row <= col

    def sums(mask):
        weights = jnp.where(mask, 1.0, 0.0).astype(bf16)
        out = jnp.dot(stacked, weights, preferred_element_type=f32)
        return [
            out[2 * heads * j : 2 * heads * j + heads] * 256.0
            + out[2 * heads * j + heads : 2 * heads * (j + 1)]
            for j in range(blocks)
        ]

    prefix = {BUCKET: sums(same & upto), LANES: sums(upto)}
    suffix = {BUCKET: sums(same & ~upto), LANES: sums(~upto)}
    total = sums(row >= 0)
    size = 2 * LANES
    while size <= tokens:
        span = size // LANES
        prefix[size], suffix[size] = [], []
        for j in range(blocks):
            start = j // span * span
            prefix[size].append(sum(total[start:j], prefix[LANES][j]))
            suffix[size].append(sum(total[j + 1 : start + span], suffix[LANES][j]))
        size *= 2
    everything = sum(total[1:], total[0])
    join = lambda pieces: jnp.concatenate(pieces, axis=1)
    return (
        {k: join(v) for k, v in prefix.items()},
        {k: join(v) for k, v in suffix.items()},
        everything,
    )


def half_order(swap):
    own = lax.axis_index("tok") if swap else 0
    return (own, 1 - own)


def start_halves(source, target, sems, dim, swap):
    extent = source.shape[dim] // 2
    copies = []
    for place, half in enumerate(half_order(swap)):
        take = [pl.ds(0, n) for n in source.shape]
        put = list(take)
        start = half * extent
        take[dim] = pl.ds(start if isinstance(start, int) else pl.multiple_of(start, extent), extent)
        put[dim] = pl.ds(place * extent, extent)
        copy = pltpu.make_async_copy(source.at[tuple(take)], target.at[tuple(put)], sems.at[place])
        copy.start()
        copies.append(copy)
    return copies


def state_kernel(pieces, order, swap, with_totals, values_hbm, keys_hbm, queries_hbm, codes_hbm, *refs):
    count = len(pieces)
    states = refs[:count]
    total_ref, turned_ref, source_ref, reader_ref, cum_ref, keys_ref, queries_ref = refs[count : count + 7]
    values_ref, codes_ref, value_sems, code_sems, row_sems = refs[count + 7 :]
    code_copies = start_halves(codes_hbm, codes_ref, code_sems, 0, swap)
    value_copies = start_halves(values_hbm, values_ref, value_sems, 1, swap)
    key_copy = pltpu.make_async_copy(keys_hbm, keys_ref, row_sems.at[0])
    key_copy.start()
    query_copy = pltpu.make_async_copy(queries_hbm, queries_ref, row_sems.at[1])
    query_copy.start()
    for copy in code_copies:
        copy.wait()
    heads, tokens = codes_ref.shape
    head_size = values_ref.shape[1] // heads
    prefix, suffix, total = decay_exponents(codes_ref[...])
    cum_ref[...] = prefix[tokens] * -decay_unit
    sizes = [BUCKET]
    while sizes[-1] * 2 < tokens:
        sizes.append(sizes[-1] * 2)
    for i, size in enumerate(sizes):
        source_ref[i] = jnp.exp(suffix[size] * -decay_unit)
    reader_ref[0] = jnp.exp(suffix[BUCKET] * decay_unit)
    for i, size in enumerate(sizes):
        reader_ref[i + 1] = jnp.exp(prefix[size] * -decay_unit)
    to_end = jnp.exp(suffix[tokens] * -decay_unit)
    total = total * -decay_unit
    total_ref[...] = total
    key_copy.wait()
    for copy in value_copies:
        copy.wait()
    keys = keys_ref[...]
    for c in order:
        first, size = pieces[c]
        low, rows = first * head_size, size * head_size
        turned = values_ref[:, low : low + rows].T
        turned_ref[low : low + rows, :] = turned
        decayed = jnp.concatenate(
            [
                (
                    turned[head_size * i : head_size * (i + 1)].astype(f32) * to_end[first + i : first + i + 1]
                ).astype(bf16)
                for i in range(size)
            ],
            axis=0,
        )
        states[c][:rows, :] = jnp.dot(decayed, keys, preferred_element_type=f32)
        if c == with_totals:
            states[c][rows:, :] = total
    query_copy.wait()


def near_kernel(
    pieces, swap, turned_ref, queries_ref, keys_ref, source_ref, decay_ref, cum_ref, weights_hbm, gain_hbm, *refs
):
    count = len(pieces)
    outs_hbm, far_ref, gain_ref = refs[:count], refs[count], refs[count + 1]
    table_ref, reader_ref, weights_ref, weight_sems, gain_sems = refs[count + 2 : count + 7]
    outs, out_sems = refs[count + 7 : -1], refs[-1]
    copies = start_halves(weights_hbm, weights_ref, weight_sems, 1, swap)
    copies += start_halves(gain_hbm, gain_ref, gain_sems, 1, swap)
    tokens = queries_ref.shape[0]
    near_levels, heads, _ = decay_ref.shape
    head_size = turned_ref.shape[0] // heads
    blocks = tokens // LANES
    row = lax.broadcasted_iota(jnp.int32, (LANES, LANES), 0)
    col = lax.broadcasted_iota(jnp.int32, (LANES, LANES), 1)
    same = (row // BUCKET) == (col // BUCKET)
    for j in range(blocks):
        span = pl.ds(LANES * j, LANES)
        scores = contract_last(keys_ref[span, :], queries_ref[span, :])
        inner = jnp.where(same & (row <= col), scores, 0.0)
        across = jnp.where(~same & (row < col), scores, 0.0)
        table_ref[j] = jnp.concatenate(split_two(jnp.concatenate([inner, across], axis=1)), axis=0)
    wide = {}
    size = LANES
    while size < tokens:
        wide[size] = []
        for start in range(0, tokens, 2 * size):
            scores = contract_last(
                keys_ref[pl.ds(start, size), :], queries_ref[pl.ds(start + size, size), :]
            )
            wide[size].append(jnp.concatenate(split_two(scores), axis=0))
        size *= 2
    for copy in copies:
        copy.wait()
    for level in range(near_levels):
        reader_ref[level] = weights_ref[level].astype(f32) * weight_unit * decay_ref[level]
    own_decay = jnp.exp(cum_ref[...])
    for slot in range(far_ref.shape[0]):
        far_ref[slot] = weights_ref[near_levels + slot].astype(f32) * weight_unit * own_decay

    stores = []
    for c, ((first, size), out) in enumerate(zip(pieces, outs)):

        def scaled(level, low, high):
            parts = []
            for h in range(first, first + size):
                part = turned_ref[pl.ds(head_size * h, head_size), low:high].astype(f32)
                parts.append((part * source_ref[level, h : h + 1, low:high]).astype(bf16))
            piece = jnp.concatenate(parts, axis=0)
            return jnp.concatenate([piece, piece], axis=1)

        def read(level, low, high, product):
            return jnp.concatenate(
                [
                    product[head_size * i : head_size * (i + 1)]
                    * reader_ref[level, first + i : first + i + 1, low:high]
                    for i in range(size)
                ],
                axis=0,
            )

        for j in range(blocks):
            low, high = LANES * j, LANES * (j + 1)
            product = jnp.dot(scaled(0, low, high), table_ref[j], preferred_element_type=f32)
            out[:, low:high] = read(0, low, high, product[:, :LANES]) + read(
                1, low, high, product[:, LANES:]
            )
        level = 2
        for span, tables in wide.items():
            for g, table in enumerate(tables):
                start = 2 * span * g
                product = jnp.dot(scaled(level - 1, start, start + span), table, preferred_element_type=f32)
                low, high = start + span, start + 2 * span
                out[:, low:high] = out[:, low:high] + read(level, low, high, product)
            level += 1
        store = pltpu.make_async_copy(out, outs_hbm[c], out_sems.at[c])
        store.start()
        stores.append(store)
    for store in stores:
        store.wait()


def finish_kernel(piece, swap, far_count, *refs):
    first, size = piece
    near_hbm, queries_ref, factor_ref, gain_ref = refs[:4]
    far_refs, gap_refs = refs[4 : 4 + far_count], refs[4 + far_count : 4 + 2 * far_count]
    out_hbm, out_ref, near_ref, sems = refs[-4:]
    load = pltpu.make_async_copy(near_hbm, near_ref, sems.at[0])
    load.start()
    rows, tokens = near_ref.shape
    heads = factor_ref.shape[1]
    head_size = rows // size
    queries = queries_ref[...]
    doubled = jnp.concatenate([queries, queries], axis=1)
    combined = [0.0] * size
    for slot in range(far_count):
        product = contract_last(jnp.concatenate(split_two(far_refs[slot][:rows, :]), axis=1), doubled)
        gap = jnp.exp(gap_refs[slot][first : first + size, :])
        factor = factor_ref[slot, first : first + size, :] * jnp.concatenate([gap] * (tokens // LANES), axis=1)
        for i in range(size):
            combined[i] = combined[i] + factor[i : i + 1] * product[head_size * i : head_size * (i + 1)]
    low = first * head_size
    gain = jnp.broadcast_to(gain_ref[0:1, low : low + rows], (LANES, rows)).T
    load.wait()
    parts = []
    for i in range(size):
        y = combined[i] + near_ref[head_size * i : head_size * (i + 1), :]
        inverse = lax.rsqrt(jnp.sum(y * y, axis=0, keepdims=True) * (1.0 / head_size) + norm_epsilon)
        own_gain = jnp.concatenate([gain[head_size * i : head_size * (i + 1)]] * (tokens // LANES), axis=1)
        parts.append((y * inverse * own_gain).astype(bf16))
    out_ref[...] = jnp.concatenate(parts, axis=0).T
    half = heads // 2
    column = half_order(swap)[first // half] * (half * head_size) + (first % half) * head_size
    if not isinstance(column, int):
        column = pl.multiple_of(column, LANES)
    store = pltpu.make_async_copy(out_ref, out_hbm.at[:, pl.ds(column, rows)], sems.at[1])
    store.start()
    store.wait()


vmem = functools.partial(pl.BlockSpec, memory_space=pltpu.VMEM)
hbm = functools.partial(pl.BlockSpec, memory_space=pltpu.HBM)
params = pltpu.CompilerParams(vmem_limit_bytes=16 * 1024 * 1024)
dma = pltpu.SemaphoreType.DMA


def in_hbm(x):
    return pltpu.with_memory_space_constraint(x, pltpu.HBM)


def spread(per_head, head_size):
    size, lanes = per_head.shape
    return jnp.broadcast_to(per_head[:, None, :], (size, head_size, lanes)).reshape(size * head_size, lanes)


def both_ways(bases, low):
    return [pair for b in bases for pair in ((b + low, b + low + 1), (b + low + 1, b + low))]


def one_way(bases, low):
    return [(b + low, b + low + 1) for b in bases]


def exchange_all(states, total, pieces, head_size):
    tok_count, seq_count = lax.axis_size("tok"), lax.axis_size("seq")
    tok_bits, seq_bits = tok_count.bit_length() - 1, seq_count.bit_length() - 1
    tok_index = lax.axis_index("tok")
    own_total, gaps = total, []
    prefix = jnp.zeros_like(total)
    aggregates, far = list(states), [[] for _ in states]
    for place in range(tok_bits):
        pairs = [(i, i ^ (1 << place)) for i in range(tok_count)]
        upper = (tok_index >> place) & 1 == 1
        partner_total = lax.ppermute(own_total, "tok", pairs)
        decay = jnp.exp(jnp.where(upper, own_total, partner_total))
        for c, (first, size) in enumerate(pieces):
            partner = lax.ppermute(aggregates[c], "tok", pairs)
            factor = spread(decay[first : first + size], head_size)
            far[c].append(partner)
            aggregates[c] = jnp.where(upper, factor * partner + aggregates[c], factor * aggregates[c] + partner)
        gaps.append(jnp.where(upper, prefix, masked_out))
        prefix = jnp.where(upper, prefix + partner_total, prefix)
        own_total = own_total + partner_total
    decay = jnp.exp(own_total)
    for place in range(seq_bits):
        half = 1 << place
        bases = range(0, seq_count, 2 * half)
        for c, (first, size) in enumerate(pieces):
            factor = spread(decay[first : first + size], head_size)
            carried = lax.ppermute(aggregates[c], "seq", [(b + half - 1, b + half) for b in bases])
            for step in range(1, half):
                carried = carried + lax.ppermute(
                    factor * carried, "seq", [(b + half + step - 1, b + half + step) for b in bases]
                )
            far[c].append(carried)
            aggregates[c] = aggregates[c] + factor * carried
        gaps.append(prefix)
    return far, gaps


def exchange_halves(states, total, pieces, head_size):
    seq_count = lax.axis_size("seq")
    seq_bits = seq_count.bit_length() - 1
    upper = lax.axis_index("tok") == 1
    seq_index = lax.axis_index("seq")
    swap = [(0, 1), (1, 0)]
    count = len(pieces) // 2
    heads = total.shape[0]
    half_heads = heads // 2
    far = [[] for _ in pieces]
    aggregates = []
    for i in range(count):
        first, size = pieces[i]
        rows = size * head_size
        received = lax.ppermute(states[count + i], "tok", swap)
        if i == 0:
            partner_total = received[rows:]
            partner_total = jnp.concatenate([partner_total[half_heads:], partner_total[:half_heads]])
            decay = jnp.exp(jnp.where(upper, total, partner_total))
        partner, own = received[:rows], states[i]
        factor = spread(decay[first : first + size], head_size)
        far[i].append(partner)
        aggregates.append(jnp.where(upper, factor * partner + own, factor * own + partner))
    for i in range(count):
        far[count + i].append(lax.ppermute(states[i], "tok", swap))
    prefix = jnp.where(upper, partner_total, 0.0)
    gaps = [jnp.where(upper, jnp.zeros_like(total), masked_out)]
    group_decay = jnp.exp(total + partner_total)
    for place in range(seq_bits):
        half = 1 << place
        bases = range(0, seq_count, 2 * half)
        for i in range(count):
            first, size = pieces[i]
            factor = spread(group_decay[first : first + size], head_size)
            first_hop = both_ways(bases, 0) if place == 0 else one_way(bases, half - 1)
            carried = lax.ppermute(aggregates[i], "seq", first_hop)
            for step in range(1, half):
                arrived = lax.ppermute(factor * carried, "seq", one_way(bases, half + step - 1))
                carried = jnp.where(seq_index % (2 * half) == half + step, arrived, carried)
            far[i].append(carried)
            far[count + i].append(lax.ppermute(carried, "tok", swap))
            aggregates[i] = aggregates[i] + factor * carried
        gaps.append(jnp.where((seq_index >> place) & 1 == 1, prefix, masked_out))
    return far, gaps


def local(values, key_rows, query_rows, decay_codes, weight_codes, norm_gain):
    heads, tokens = decay_codes.shape
    columns = values.shape[1]
    head_size = columns // heads
    state_size = key_rows.shape[1]
    near_levels = (tokens // BUCKET).bit_length()
    far_count = lax.axis_size("tok").bit_length() + lax.axis_size("seq").bit_length() - 2
    swap = lax.axis_size("tok") == 2
    half = heads // 2
    count = PIECES
    size = half // count
    pieces = [(size * i, size) for i in range(2 * count)]
    order = [*range(count, 2 * count), *range(count)]
    with_totals = count if swap else None

    *states, total, turned, source, decay, cum, keys, queries = pl.pallas_call(
        functools.partial(state_kernel, pieces, order, swap, with_totals),
        name="state",
        out_shape=[
            jax.ShapeDtypeStruct((n * head_size + (heads if c == with_totals else 0), state_size), f32)
            for c, (_, n) in enumerate(pieces)
        ]
        + [
            jax.ShapeDtypeStruct((heads, LANES), f32),
            jax.ShapeDtypeStruct((columns, tokens), bf16),
            jax.ShapeDtypeStruct((near_levels - 1, heads, tokens), f32),
            jax.ShapeDtypeStruct((near_levels, heads, tokens), f32),
            jax.ShapeDtypeStruct((heads, tokens), f32),
            jax.ShapeDtypeStruct(key_rows.shape, key_rows.dtype),
            jax.ShapeDtypeStruct(query_rows.shape, query_rows.dtype),
        ],
        in_specs=[hbm()] * 4,
        out_specs=[vmem()] * (len(pieces) + 7),
        scratch_shapes=[
            pltpu.VMEM(values.shape, values.dtype),
            pltpu.VMEM(decay_codes.shape, decay_codes.dtype),
            dma((2,)),
            dma((2,)),
            dma((2,)),
        ],
        compiler_params=params,
    )(*(in_hbm(x) for x in (values, key_rows, query_rows, decay_codes)))

    near_call = pl.pallas_call(
        functools.partial(near_kernel, pieces, swap),
        name="near",
        out_shape=[pltpu.HBM((n * head_size, tokens), f32) for _, n in pieces]
        + [
            jax.ShapeDtypeStruct((far_count, heads, tokens), f32),
            jax.ShapeDtypeStruct((1, columns), f32),
        ],
        in_specs=[vmem()] * 6 + [hbm()] * 2,
        out_specs=[hbm()] * len(pieces) + [vmem()] * 2,
        scratch_shapes=[
            pltpu.VMEM((tokens // LANES, 2 * LANES, 2 * LANES), bf16),
            pltpu.VMEM((near_levels, heads, tokens), f32),
            pltpu.VMEM(weight_codes.shape, weight_codes.dtype),
            dma((2,)),
            dma((2,)),
        ]
        + [pltpu.VMEM((n * head_size, tokens), f32) for _, n in pieces]
        + [dma((len(pieces),))],
        compiler_params=params,
    )
    *near, far_factor, gain = near_call(
        turned, queries, keys, source, decay, cum, in_hbm(weight_codes), in_hbm(norm_gain.reshape(1, columns))
    )

    exchange = exchange_halves if swap else exchange_all
    far, gaps = exchange(states, total, pieces, head_size)
    out = None
    for c, piece in enumerate(pieces):
        rows = piece[1] * head_size
        operands = [near[c], queries, far_factor, gain, *far[c], *gaps]
        in_specs = [hbm()] + [vmem()] * (len(operands) - 1)
        aliases = {}
        if out is not None:
            aliases = {len(operands): 0}
            operands.append(out)
            in_specs.append(hbm())
        finish_call = pl.pallas_call(
            functools.partial(finish_kernel, piece, swap, far_count),
            out_shape=pltpu.HBM((tokens, columns), bf16),
            in_specs=in_specs,
            out_specs=hbm(),
            scratch_shapes=[pltpu.VMEM((tokens, rows), bf16), pltpu.VMEM((rows, tokens), f32), dma((2,))],
            input_output_aliases=aliases,
            compiler_params=params,
        )
        out = finish_call(*operands)
    return out


def solution(mesh):
    return jax.shard_map(
        local,
        mesh=mesh,
        in_specs=(
            P(("parts", "seq", "tok"), "head"),
            P(("parts", "seq", "tok"), None),
            P(("parts", "seq", "tok"), None),
            P("head", ("parts", "seq", "tok")),
            P(None, "head", ("parts", "seq", "tok")),
            P("head"),
        ),
        out_specs=P(("parts", "seq", "tok"), "head"),
        check_vma=False,
    )
```

time: 57.7 us -> 47.2 us (0.82)
  the two profiles are of different devices: /device:TPU:22 before, /device:TPU:26 now
where the time goes in v2:
time: 47.2 us; the launch traced here: 47 us
  waiting for transfers between devices  21.1 us (45%)
  starting transfers between devices  13.3 us (28%)
  Pallas kernels  11.2 us (24%)
  local copies, waits for them, and re-layouts  1.07 us (2%)
    ppermute x2, waiting for transfers between devices, exchange_halves(): lax.ppermute(factor * carried, 'seq', one_way(bases, half + step - 1))  10.8 us
    ppermute x2, waiting for transfers between devices, exchange_halves(): received = lax.ppermute(states[count + i], 'tok', swap)  5.61 us
    pallas_call x4, Pallas kernels, local(): out = finish_call(*operands)  5.43 us
    ppermute x4, waiting for transfers between devices, exchange_halves(): carried = lax.ppermute(aggregates[i], 'seq', first_hop)  4.6 us
    ppermute x4, starting transfers between devices, exchange_halves(): far[count + i].append(lax.ppermute(carried, 'tok', swap))  4.12 us
    pallas_call x1, Pallas kernels, local(): near_call(turned, queries, keys, source, decay, cum, in_hbm(weight_codes)...  3.82 us
    ppermute x2, starting transfers between devices, exchange_halves(): lax.ppermute(factor * carried, 'seq', one_way(bases, half + step - 1))  2.57 us
    ppermute x4, starting transfers between devices, exchange_halves(): carried = lax.ppermute(aggregates[i], 'seq', first_hop)  2.41 us
  transfers between devices with their start and end apart: 14, of which 6 were waited for; matrix products, arithmetic and copies ran while one was open for 0% of the time, Pallas kernels for 17%

profile of v2, /device:TPU:26, one launch (start us, length us, event | category | flops | bytes accessed | tf_op | source)
XLA Modules:
  0.0 47.0 jit_solution(1619374502857768591)
XLA Ops:
  0.0 2.0 %state.1 = (f32[256,128]{1,0:T(8,128)S(1)}, f32[256,128]{1,0:T(8,128)S(1)}, f32[272,128]{1,0:T(8,128)S(1)}, f32[256,128]{1,0:T(8,128)S(1)}, f32[16,128]{1,0:T(8,...) custom-call(bf16[512,1024]{1,0:T(8,128)(2,1)} %values_hbm.1, ...), custom_call_target="tpu_custom_call" | custom-call | tf_op jit(solution)/shard_map/state/pallas_call | solution.py:389
  2.0 0.6 %collective-permute-start.1 = (f32[272,128]{1,0:T(8,128)S(1)}, f32[272,128]{1,0:T(8,128)S(1)}, u32[]{:S(2)}, u32[]{:S(2)}) collective-permute-start(f32[272,128]{1,0:T(8,128)S(1)} %get-tuple-element.33), channel_id=1, source_target_pairs={{0,2},{2,0},{1,3},{3,1},{4,6},{6,4},{5,7},{7,5},{8,10},{10,8},{9,1... | collective-permute-start | bytes 417800 | tf_op jit(solution)/shard_map/ppermute | solution.py:342
  2.6 1.5 %collective-permute-start.2 = (f32[256,128]{1,0:T(8,128)S(1)}, f32[256,128]{1,0:T(8,128)S(1)}, u32[]{:S(2)}, u32[]{:S(2)}) collective-permute-start(f32[256,128]{1,0:T(8,128)S(1)} %get-tuple-element.34), channel_id=1, source_target_pairs={{0,2},{2,0},{1,3},{3,1},{4,6},{6,4},{5,7},{7,5},{8,10},{10,8},{9,1... | collective-permute-start | bytes 393224 | tf_op jit(solution)/shard_map/ppermute | solution.py:342
  4.1 4.5 %collective-permute-done.1 = f32[272,128]{1,0:T(8,128)S(1)} collective-permute-done((f32[272,128]{1,0:T(8,128)S(1)}, f32[272,128]{1,0:T(8,128)S(1)}, u32[]{:S(2)}, u32[]{:S(2)}) %collective-permute-start.1) | collective-permute-done | bytes 139296 | tf_op jit(solution)/shard_map/ppermute | solution.py:342
  8.6 0.5 %collective-permute-start.9 = (f32[256,128]{1,0:T(8,128)S(1)}, f32[256,128]{1,0:T(8,128)S(1)}, u32[]{:S(2)}, u32[]{:S(2)}) collective-permute-start(f32[256,128]{1,0:T(8,128)S(1)} %get-tuple-element.40), channel_id=1, source_target_pairs={{0,4},{4,0},{8,12},{12,8},{1,5},{5,1},{9,13},{13,9},{2,6},{6,2},{1... | collective-permute-start | bytes 393224 | tf_op jit(solution)/shard_map/ppermute | solution.py:363
  9.2 1.1 %collective-permute-done.2.refs_4_ = f32[256,128]{1,0:T(8,128)S(1)} collective-permute-done((f32[256,128]{1,0:T(8,128)S(1)}, f32[256,128]{1,0:T(8,128)S(1)}, u32[]{:S(2)}, u32[]{:S(2)}) %collective-permute-start.2) | collective-permute-done | bytes 131104 | tf_op jit(solution)/shard_map/ppermute | solution.py:342
  10.3 0.6 %collective-permute-start.3 = (f32[256,128]{1,0:T(8,128)S(1)}, f32[256,128]{1,0:T(8,128)S(1)}, u32[]{:S(2)}, u32[]{:S(2)}) collective-permute-start(f32[256,128]{1,0:T(8,128)S(1)} %fusion.1), channel_id=1, source_target_pairs={{0,4},{4,0},{8,12},{12,8},{1,5},{5,1},{9,13},{13,9},{2,6},{6,2},{1... | collective-permute-start | bytes 393224 | tf_op jit(solution)/shard_map/ppermute | solution.py:363
  10.8 3.9 %collective-permute-done.9.refs_5_ = f32[256,128]{1,0:T(8,128)S(1)} collective-permute-done((f32[256,128]{1,0:T(8,128)S(1)}, f32[256,128]{1,0:T(8,128)S(1)}, u32[]{:S(2)}, u32[]{:S(2)}) %collective-permute-start.9) | collective-permute-done | bytes 131104 | tf_op jit(solution)/shard_map/ppermute | solution.py:363
  14.7 0.7 %collective-permute-start.11 = (f32[256,128]{1,0:T(8,128)S(1)}, f32[256,128]{1,0:T(8,128)S(1)}, u32[]{:S(2)}, u32[]{:S(2)}) collective-permute-start(f32[256,128]{1,0:T(8,128)S(1)} %fusion.7), channel_id=1, source_target_pairs={{4,8},{5,9},{6,10},{7,11},{20,24},{21,25},{22,26},{23,27}} | collective-permute-start | bytes 393224 | tf_op jit(solution)/shard_map/ppermute | solution.py:363
  15.4 0.7 %collective-permute-done.3.refs_5_ = f32[256,128]{1,0:T(8,128)S(1)} collective-permute-done((f32[256,128]{1,0:T(8,128)S(1)}, f32[256,128]{1,0:T(8,128)S(1)}, u32[]{:S(2)}, u32[]{:S(2)}) %collective-permute-start.3) | collective-permute-done | bytes 131104 | tf_op jit(solution)/shard_map/ppermute | solution.py:363
  16.2 0.7 %collective-permute-start.5 = (f32[256,128]{1,0:T(8,128)S(1)}, f32[256,128]{1,0:T(8,128)S(1)}, u32[]{:S(2)}, u32[]{:S(2)}) collective-permute-start(f32[256,128]{1,0:T(8,128)S(1)} %fusion.3), channel_id=1, source_target_pairs={{4,8},{5,9},{6,10},{7,11},{20,24},{21,25},{22,26},{23,27}} | collective-permute-start | bytes 393224 | tf_op jit(solution)/shard_map/ppermute | solution.py:363
  16.8 0.0 collective-permute-done.11
  16.9 1.3 %collective-permute-start.12 = (f32[256,128]{1,0:T(8,128)S(1)}, f32[256,128]{1,0:T(8,128)S(1)}, u32[]{:S(2)}, u32[]{:S(2)}) collective-permute-start(f32[256,128]{1,0:T(8,128)S(1)} %bitcast_multiply_fusion), channel_id=1, source_target_pairs={{8,12},{9,13},{10,14},{11,15},{24,28},{25,29},{26,30},{27,31}} | collective-permute-start | bytes 393224 | tf_op jit(solution)/shard_map/ppermute | solution.py:365
  18.2 0.6 %collective-permute-start.8 = (f32[256,128]{1,0:T(8,128)S(1)}, f32[256,128]{1,0:T(8,128)S(1)}, u32[]{:S(2)}, u32[]{:S(2)}) collective-permute-start(f32[256,128]{1,0:T(8,128)S(1)} %get-tuple-element.36), channel_id=1, source_target_pairs={{0,2},{2,0},{1,3},{3,1},{4,6},{6,4},{5,7},{7,5},{8,10},{10,8},{9,1... | collective-permute-start | bytes 393224 | tf_op jit(solution)/shard_map/ppermute | solution.py:352
  18.8 1.5 %collective-permute-start = (f32[256,128]{1,0:T(8,128)S(1)}, f32[256,128]{1,0:T(8,128)S(1)}, u32[]{:S(2)}, u32[]{:S(2)}) collective-permute-start(f32[256,128]{1,0:T(8,128)S(1)} %get-tuple-element.31), channel_id=1, source_target_pairs={{0,2},{2,0},{1,3},{3,1},{4,6},{6,4},{5,7},{7,5},{8,10},{10,8},{9,1... | collective-permute-start | bytes 393224 | tf_op jit(solution)/shard_map/ppermute | solution.py:352
  20.3 0.5 %collective-permute-start.10 = (f32[256,128]{1,0:T(8,128)S(1)}, f32[256,128]{1,0:T(8,128)S(1)}, u32[]{:S(2)}, u32[]{:S(2)}) collective-permute-start(f32[256,128]{1,0:T(8,128)S(1)} %collective-permute-done.9.refs_5_), channel_id=1, source_target_pairs={{0,2},{2,0},{1,3},{3,1},{4,6},{6,4},{5,7},{7,5},{8,10},{10,8},{9,1... | collective-permute-start | bytes 393224 | tf_op jit(solution)/shard_map/ppermute | solution.py:368
  20.8 0.0 collective-permute-done.5
  20.8 1.5 %collective-permute-start.4 = (f32[256,128]{1,0:T(8,128)S(1)}, f32[256,128]{1,0:T(8,128)S(1)}, u32[]{:S(2)}, u32[]{:S(2)}) collective-permute-start(f32[256,128]{1,0:T(8,128)S(1)} %collective-permute-done.3.refs_5_), channel_id=1, source_target_pairs={{0,2},{2,0},{1,3},{3,1},{4,6},{6,4},{5,7},{7,5},{8,10},{10,8},{9,1... | collective-permute-start | bytes 393224 | tf_op jit(solution)/shard_map/ppermute | solution.py:368
  22.3 5.3 %collective-permute-done.12 = f32[256,128]{1,0:T(8,128)S(1)} collective-permute-done((f32[256,128]{1,0:T(8,128)S(1)}, f32[256,128]{1,0:T(8,128)S(1)}, u32[]{:S(2)}, u32[]{:S(2)}) %collective-permute-start.12) | collective-permute-done | bytes 131104 | tf_op jit(solution)/shard_map/ppermute | solution.py:365
  27.6 1.3 %collective-permute-start.6 = (f32[256,128]{1,0:T(8,128)S(1)}, f32[256,128]{1,0:T(8,128)S(1)}, u32[]{:S(2)}, u32[]{:S(2)}) collective-permute-start(f32[256,128]{1,0:T(8,128)S(1)} %bitcast_multiply_fusion.4), channel_id=1, source_target_pairs={{8,12},{9,13},{10,14},{11,15},{24,28},{25,29},{26,30},{27,31}} | collective-permute-start | bytes 393224 | tf_op jit(solution)/shard_map/ppermute | solution.py:365
  28.9 5.5 %collective-permute-done.6 = f32[256,128]{1,0:T(8,128)S(1)} collective-permute-done((f32[256,128]{1,0:T(8,128)S(1)}, f32[256,128]{1,0:T(8,128)S(1)}, u32[]{:S(2)}, u32[]{:S(2)}) %collective-permute-start.6) | collective-permute-done | bytes 131104 | tf_op jit(solution)/shard_map/ppermute | solution.py:365
  34.4 0.5 %collective-permute-start.13 = (f32[256,128]{1,0:T(8,128)S(1)}, f32[256,128]{1,0:T(8,128)S(1)}, u32[]{:S(2)}, u32[]{:S(2)}) collective-permute-start(f32[256,128]{1,0:T(8,128)S(1)} %broadcast_select_fusion.refs_6_), channel_id=1, source_target_pairs={{0,2},{2,0},{1,3},{3,1},{4,6},{6,4},{5,7},{7,5},{8,10},{10,8},{9,1... | collective-permute-start | bytes 393224 | tf_op jit(solution)/shard_map/ppermute | solution.py:368
  35.0 0.0 collective-permute-done.8.refs_4_
  35.0 1.6 %collective-permute-start.7 = (f32[256,128]{1,0:T(8,128)S(1)}, f32[256,128]{1,0:T(8,128)S(1)}, u32[]{:S(2)}, u32[]{:S(2)}) collective-permute-start(f32[256,128]{1,0:T(8,128)S(1)} %broadcast_select_fusion.1.refs_6_), channel_id=1, source_target_pairs={{0,2},{2,0},{1,3},{3,1},{4,6},{6,4},{5,7},{7,5},{8,10},{10,8},{9,1... | collective-permute-start | bytes 393224 | tf_op jit(solution)/shard_map/ppermute | solution.py:368
  36.6 3.8 %near.1 = (f32[256,512]{1,0:T(8,128)}, f32[256,512]{1,0:T(8,128)}, f32[256,512]{1,0:T(8,128)}, f32[256,512]{1,0:T(8,128)}, f32[3,16,512]{2,1,0:T(8,128)S(1)}, /*index=5*/f32[1,1024]{1,0:T(1,128)S(1)}) custom-call(bf16[1024,512]{1,0:T(8,128)(2,1)S(1)} %get-tuple-element.22.turned_ref, bf16[512,128]{1,0:T(8,128)(2,1)S(1)} %get-tuple-element.23.queries_ref.refs_1_, ...), custom_call_target="tpu_custom_call" | custom-call | tf_op jit(solution)/shard_map/near/pallas_call | solution.py:438
  40.4 0.0 copy-start.3
  40.4 1.0 %copy-done.3 = f32[256,512]{1,0:T(8,128)S(1)} copy-done((f32[256,512]{1,0:T(8,128)S(1)}, f32[256,512]{1,0:T(8,128)}, u32[]{:S(2)}) %copy-start.3) | copy-done | bytes 524312
  41.4 0.0 copy-start.2
  41.4 1.4 %shard_map.64.refs_10_ = bf16[512,1024]{1,0:T(8,128)(2,1)} custom-call(f32[256,512]{1,0:T(8,128)S(1)} %copy-done.3, bf16[512,128]{1,0:T(8,128)(2,1)S(1)} %get-tuple-element.23.queries_ref.refs_1_, f32[3,16,512]{2,1,0:T(8,128)S(1)} %get-tuple-element.29.refs_2_, f32[1,1024]{1,0:T(1,128)S(1)} %get-tuple-element.30.refs_3_, ...), custom_call_target="tpu_custom_call" | custom-call | tf_op jit(solution)/shard_map/pallas_call | solution.py:463
  42.8 0.0 copy-done.2
  42.8 0.0 copy-start.1
  42.8 1.4 %shard_map.65.refs_10_ = bf16[512,1024]{1,0:T(8,128)(2,1)} custom-call(f32[256,512]{1,0:T(8,128)S(1)} %copy-done.2, bf16[512,128]{1,0:T(8,128)(2,1)S(1)} %get-tuple-element.23.queries_ref.refs_1_, f32[3,16,512]{2,1,0:T(8,128)S(1)} %get-tuple-element.29.refs_2_, f32[1,1024]{1,0:T(1,128)S(1)} %get-tuple-element.30.refs_3_, ...), custom_call_target="tpu_custom_call", output_to_operand_aliasing={{}: (10, {})} | custom-call | tf_op jit(solution)/shard_map/pallas_call | solution.py:463
  44.2 0.0 collective-permute-done.10.refs_5_
  44.2 0.0 collective-permute-done.13.refs_6_
  44.2 0.0 copy-done.1
  44.2 0.0 copy-start
  44.2 1.4 %shard_map.66.refs_10_ = bf16[512,1024]{1,0:T(8,128)(2,1)} custom-call(f32[256,512]{1,0:T(8,128)S(1)} %copy-done.1, bf16[512,128]{1,0:T(8,128)(2,1)S(1)} %get-tuple-element.23.queries_ref.refs_1_, f32[3,16,512]{2,1,0:T(8,128)S(1)} %get-tuple-element.29.refs_2_, f32[1,1024]{1,0:T(1,128)S(1)} %get-tuple-element.30.refs_3_, ...), custom_call_target="tpu_custom_call", output_to_operand_aliasing={{}: (10, {})} | custom-call | tf_op jit(solution)/shard_map/pallas_call | solution.py:463
  45.6 0.0 collective-permute-done.refs_4_
  45.6 0.0 collective-permute-done.4.refs_5_
  45.6 0.0 collective-permute-done.7.refs_6_
  45.6 0.0 copy-done
  45.6 1.4 %shard_map.67 = bf16[512,1024]{1,0:T(8,128)(2,1)} custom-call(f32[256,512]{1,0:T(8,128)S(1)} %copy-done, bf16[512,128]{1,0:T(8,128)(2,1)S(1)} %get-tuple-element.23.queries_ref.refs_1_, f32[3,16,512]{2,1,0:T(8,128)S(1)} %get-tuple-element.29.refs_2_, f32[1,1024]{1,0:T(1,128)S(1)} %get-tuple-element.30.refs_3_, ...), custom_call_target="tpu_custom_call", output_to_operand_aliasing={{}: (10, {})} | custom-call | tf_op jit(solution)/shard_map/pallas_call | solution.py:463
  (13 shorter events, 0.2 us)
Async XLA Ops:
  2.0 6.6 %collective-permute-start.1 = (f32[272,128]{1,0:T(8,128)S(1)}, f32[272,128]{1,0:T(8,128)S(1)}, u32[]{:S(2)}, u32[]{:S(2)}) collective-permute-start(f32[272,128]{1,0:T(8,128)S(1)} %get-tuple-element.33), channel_id=1, source_target_pairs={{0,2},{2,0},{1,3},{3,1},{4,6},{6,4},{5,7},{7,5},{8,10},{10,8},{9,1... | collective-permute-start | bytes 417800 | tf_op jit(solution)/shard_map/ppermute | solution.py:342
  2.6 7.7 %collective-permute-start.2 = (f32[256,128]{1,0:T(8,128)S(1)}, f32[256,128]{1,0:T(8,128)S(1)}, u32[]{:S(2)}, u32[]{:S(2)}) collective-permute-start(f32[256,128]{1,0:T(8,128)S(1)} %get-tuple-element.34), channel_id=1, source_target_pairs={{0,2},{2,0},{1,3},{3,1},{4,6},{6,4},{5,7},{7,5},{8,10},{10,8},{9,1... | collective-permute-start | bytes 393224 | tf_op jit(solution)/shard_map/ppermute | solution.py:342
  8.6 6.1 %collective-permute-start.9 = (f32[256,128]{1,0:T(8,128)S(1)}, f32[256,128]{1,0:T(8,128)S(1)}, u32[]{:S(2)}, u32[]{:S(2)}) collective-permute-start(f32[256,128]{1,0:T(8,128)S(1)} %get-tuple-element.40), channel_id=1, source_target_pairs={{0,4},{4,0},{8,12},{12,8},{1,5},{5,1},{9,13},{13,9},{2,6},{6,2},{1... | collective-permute-start | bytes 393224 | tf_op jit(solution)/shard_map/ppermute | solution.py:363
  10.3 5.8 %collective-permute-start.3 = (f32[256,128]{1,0:T(8,128)S(1)}, f32[256,128]{1,0:T(8,128)S(1)}, u32[]{:S(2)}, u32[]{:S(2)}) collective-permute-start(f32[256,128]{1,0:T(8,128)S(1)} %fusion.1), channel_id=1, source_target_pairs={{0,4},{4,0},{8,12},{12,8},{1,5},{5,1},{9,13},{13,9},{2,6},{6,2},{1... | collective-permute-start | bytes 393224 | tf_op jit(solution)/shard_map/ppermute | solution.py:363
  14.7 2.1 %collective-permute-start.11 = (f32[256,128]{1,0:T(8,128)S(1)}, f32[256,128]{1,0:T(8,128)S(1)}, u32[]{:S(2)}, u32[]{:S(2)}) collective-permute-start(f32[256,128]{1,0:T(8,128)S(1)} %fusion.7), channel_id=1, source_target_pairs={{4,8},{5,9},{6,10},{7,11},{20,24},{21,25},{22,26},{23,27}} | collective-permute-start | bytes 393224 | tf_op jit(solution)/shard_map/ppermute | solution.py:363
  16.2 4.6 %collective-permute-start.5 = (f32[256,128]{1,0:T(8,128)S(1)}, f32[256,128]{1,0:T(8,128)S(1)}, u32[]{:S(2)}, u32[]{:S(2)}) collective-permute-start(f32[256,128]{1,0:T(8,128)S(1)} %fusion.3), channel_id=1, source_target_pairs={{4,8},{5,9},{6,10},{7,11},{20,24},{21,25},{22,26},{23,27}} | collective-permute-start | bytes 393224 | tf_op jit(solution)/shard_map/ppermute | solution.py:363
  16.9 10.7 %collective-permute-start.12 = (f32[256,128]{1,0:T(8,128)S(1)}, f32[256,128]{1,0:T(8,128)S(1)}, u32[]{:S(2)}, u32[]{:S(2)}) collective-permute-start(f32[256,128]{1,0:T(8,128)S(1)} %bitcast_multiply_fusion), channel_id=1, source_target_pairs={{8,12},{9,13},{10,14},{11,15},{24,28},{25,29},{26,30},{27,31}} | collective-permute-start | bytes 393224 | tf_op jit(solution)/shard_map/ppermute | solution.py:365
  18.2 16.8 %collective-permute-start.8 = (f32[256,128]{1,0:T(8,128)S(1)}, f32[256,128]{1,0:T(8,128)S(1)}, u32[]{:S(2)}, u32[]{:S(2)}) collective-permute-start(f32[256,128]{1,0:T(8,128)S(1)} %get-tuple-element.36), channel_id=1, source_target_pairs={{0,2},{2,0},{1,3},{3,1},{4,6},{6,4},{5,7},{7,5},{8,10},{10,8},{9,1... | collective-permute-start | bytes 393224 | tf_op jit(solution)/shard_map/ppermute | solution.py:352
  18.8 26.8 %collective-permute-start = (f32[256,128]{1,0:T(8,128)S(1)}, f32[256,128]{1,0:T(8,128)S(1)}, u32[]{:S(2)}, u32[]{:S(2)}) collective-permute-start(f32[256,128]{1,0:T(8,128)S(1)} %get-tuple-element.31), channel_id=1, source_target_pairs={{0,2},{2,0},{1,3},{3,1},{4,6},{6,4},{5,7},{7,5},{8,10},{10,8},{9,1... | collective-permute-start | bytes 393224 | tf_op jit(solution)/shard_map/ppermute | solution.py:352
  20.3 23.9 %collective-permute-start.10 = (f32[256,128]{1,0:T(8,128)S(1)}, f32[256,128]{1,0:T(8,128)S(1)}, u32[]{:S(2)}, u32[]{:S(2)}) collective-permute-start(f32[256,128]{1,0:T(8,128)S(1)} %collective-permute-done.9.refs_5_), channel_id=1, source_target_pairs={{0,2},{2,0},{1,3},{3,1},{4,6},{6,4},{5,7},{7,5},{8,10},{10,8},{9,1... | collective-permute-start | bytes 393224 | tf_op jit(solution)/shard_map/ppermute | solution.py:368
  20.8 24.8 %collective-permute-start.4 = (f32[256,128]{1,0:T(8,128)S(1)}, f32[256,128]{1,0:T(8,128)S(1)}, u32[]{:S(2)}, u32[]{:S(2)}) collective-permute-start(f32[256,128]{1,0:T(8,128)S(1)} %collective-permute-done.3.refs_5_), channel_id=1, source_target_pairs={{0,2},{2,0},{1,3},{3,1},{4,6},{6,4},{5,7},{7,5},{8,10},{10,8},{9,1... | collective-permute-start | bytes 393224 | tf_op jit(solution)/shard_map/ppermute | solution.py:368
  27.6 6.8 %collective-permute-start.6 = (f32[256,128]{1,0:T(8,128)S(1)}, f32[256,128]{1,0:T(8,128)S(1)}, u32[]{:S(2)}, u32[]{:S(2)}) collective-permute-start(f32[256,128]{1,0:T(8,128)S(1)} %bitcast_multiply_fusion.4), channel_id=1, source_target_pairs={{8,12},{9,13},{10,14},{11,15},{24,28},{25,29},{26,30},{27,31}} | collective-permute-start | bytes 393224 | tf_op jit(solution)/shard_map/ppermute | solution.py:365
  34.4 9.8 %collective-permute-start.13 = (f32[256,128]{1,0:T(8,128)S(1)}, f32[256,128]{1,0:T(8,128)S(1)}, u32[]{:S(2)}, u32[]{:S(2)}) collective-permute-start(f32[256,128]{1,0:T(8,128)S(1)} %broadcast_select_fusion.refs_6_), channel_id=1, source_target_pairs={{0,2},{2,0},{1,3},{3,1},{4,6},{6,4},{5,7},{7,5},{8,10},{10,8},{9,1... | collective-permute-start | bytes 393224 | tf_op jit(solution)/shard_map/ppermute | solution.py:368
  35.0 10.6 %collective-permute-start.7 = (f32[256,128]{1,0:T(8,128)S(1)}, f32[256,128]{1,0:T(8,128)S(1)}, u32[]{:S(2)}, u32[]{:S(2)}) collective-permute-start(f32[256,128]{1,0:T(8,128)S(1)} %broadcast_select_fusion.1.refs_6_), channel_id=1, source_target_pairs={{0,2},{2,0},{1,3},{3,1},{4,6},{6,4},{5,7},{7,5},{8,10},{10,8},{9,1... | collective-permute-start | bytes 393224 | tf_op jit(solution)/shard_map/ppermute | solution.py:368
  40.4 1.0 %copy-start.3 = (f32[256,512]{1,0:T(8,128)S(1)}, f32[256,512]{1,0:T(8,128)}, u32[]{:S(2)}) copy-start(f32[256,512]{1,0:T(8,128)} %get-tuple-element.38.refs_0_) | copy-start | bytes 1572868
  41.4 1.4 %copy-start.2 = (f32[256,512]{1,0:T(8,128)S(1)}, f32[256,512]{1,0:T(8,128)}, u32[]{:S(2)}) copy-start(f32[256,512]{1,0:T(8,128)} %get-tuple-element.37.refs_0_) | copy-start | bytes 1572868
  42.8 1.4 %copy-start.1 = (f32[256,512]{1,0:T(8,128)S(1)}, f32[256,512]{1,0:T(8,128)}, u32[]{:S(2)}) copy-start(f32[256,512]{1,0:T(8,128)} %get-tuple-element.35.refs_0_) | copy-start | bytes 1572868
  44.2 1.4 %copy-start = (f32[256,512]{1,0:T(8,128)S(1)}, f32[256,512]{1,0:T(8,128)}, u32[]{:S(2)}) copy-start(f32[256,512]{1,0:T(8,128)} %get-tuple-element.28.refs_0_) | copy-start | bytes 1572868

commit v3 on v2

--- a/solution.py
+++ b/solution.py
@@ -10,7 +10,7 @@
 
 BUCKET = 64
 LANES = 128
-PIECES = 2
+PIECE_SHARES = (1, 1)
 
 decay_unit = 1.0 / 65536.0
 weight_unit = 1.0 / 256.0
@@ -78,36 +78,49 @@
     return (own, 1 - own)
 
 
+def start_half(source, target, sem, dim, half):
+    extent = source.shape[dim] // 2
+    take = [pl.ds(0, n) for n in source.shape]
+    start = half * extent
+    take[dim] = pl.ds(start if isinstance(start, int) else pl.multiple_of(start, extent), extent)
+    copy = pltpu.make_async_copy(source.at[tuple(take)], target, sem)
+    copy.start()
+    return copy
+
+
 def start_halves(source, target, sems, dim, swap):
     extent = source.shape[dim] // 2
     copies = []
     for place, half in enumerate(half_order(swap)):
-        take = [pl.ds(0, n) for n in source.shape]
-        put = list(take)
-        start = half * extent
-        take[dim] = pl.ds(start if isinstance(start, int) else pl.multiple_of(start, extent), extent)
+        put = [pl.ds(0, n) for n in source.shape]
         put[dim] = pl.ds(place * extent, extent)
-        copy = pltpu.make_async_copy(source.at[tuple(take)], target.at[tuple(put)], sems.at[place])
-        copy.start()
-        copies.append(copy)
+        copies.append(start_half(source, target.at[tuple(put)], sems.at[place], dim, half))
     return copies
 
 
-def state_kernel(pieces, order, swap, with_totals, values_hbm, keys_hbm, queries_hbm, codes_hbm, *refs):
-    count = len(pieces)
+def decayed_state(turned, to_end, keys, first, size, base):
+    head_size = turned.shape[0] // (to_end.shape[0] // 2)
+    parts = []
+    for h in range(first, first + size):
+        row = (h - base) * head_size
+        parts.append((turned[row : row + head_size].astype(f32) * to_end[h : h + 1]).astype(bf16))
+    return jnp.dot(jnp.concatenate(parts, axis=0), keys, preferred_element_type=f32)
+
+
+def state_kernel(pieces, swap, values_hbm, keys_hbm, queries_hbm, codes_hbm, *refs):
+    count = len(pieces) // 2
     states = refs[:count]
-    total_ref, turned_ref, source_ref, reader_ref, cum_ref, keys_ref, queries_ref = refs[count : count + 7]
-    values_ref, codes_ref, value_sems, code_sems, row_sems = refs[count + 7 :]
+    total_ref, turned_ref, source_ref, reader_ref, cum_ref, end_ref, keys_ref, queries_ref = refs[count : count + 8]
+    values_ref, codes_ref, code_sems, row_sems = refs[count + 8 :]
     code_copies = start_halves(codes_hbm, codes_ref, code_sems, 0, swap)
-    value_copies = start_halves(values_hbm, values_ref, value_sems, 1, swap)
     key_copy = pltpu.make_async_copy(keys_hbm, keys_ref, row_sems.at[0])
     key_copy.start()
-    query_copy = pltpu.make_async_copy(queries_hbm, queries_ref, row_sems.at[1])
+    value_copy = start_half(values_hbm, values_ref, row_sems.at[1], 1, half_order(swap)[1])
+    query_copy = pltpu.make_async_copy(queries_hbm, queries_ref, row_sems.at[2])
     query_copy.start()
     for copy in code_copies:
         copy.wait()
     heads, tokens = codes_ref.shape
-    head_size = values_ref.shape[1] // heads
     prefix, suffix, total = decay_exponents(codes_ref[...])
     cum_ref[...] = prefix[tokens] * -decay_unit
     sizes = [BUCKET]
@@ -119,44 +132,50 @@
     for i, size in enumerate(sizes):
         reader_ref[i + 1] = jnp.exp(prefix[size] * -decay_unit)
     to_end = jnp.exp(suffix[tokens] * -decay_unit)
+    end_ref[...] = to_end
     total = total * -decay_unit
     total_ref[...] = total
     key_copy.wait()
-    for copy in value_copies:
-        copy.wait()
+    value_copy.wait()
     keys = keys_ref[...]
-    for c in order:
-        first, size = pieces[c]
-        low, rows = first * head_size, size * head_size
-        turned = values_ref[:, low : low + rows].T
-        turned_ref[low : low + rows, :] = turned
-        decayed = jnp.concatenate(
-            [
-                (
-                    turned[head_size * i : head_size * (i + 1)].astype(f32) * to_end[first + i : first + i + 1]
-                ).astype(bf16)
-                for i in range(size)
-            ],
-            axis=0,
-        )
-        states[c][:rows, :] = jnp.dot(decayed, keys, preferred_element_type=f32)
-        if c == with_totals:
-            states[c][rows:, :] = total
+    head_size = 2 * values_ref.shape[1] // heads
+    base = pieces[count][0]
+    for state_ref, (first, size) in zip(states, pieces[count:]):
+        low, rows = (first - base) * head_size, size * head_size
+        turned_ref[low : low + rows, :] = values_ref[:, low : low + rows].T
+        state_ref[:rows, :] = decayed_state(turned_ref, to_end, keys, first, size, base)
+        if state_ref.shape[0] > rows:
+            state_ref[rows:, :] = total
     query_copy.wait()
 
 
 def near_kernel(
-    pieces, swap, turned_ref, queries_ref, keys_ref, source_ref, decay_ref, cum_ref, weights_hbm, gain_hbm, *refs
+    pieces,
+    swap,
+    own_splits,
+    other_ref,
+    queries_ref,
+    keys_ref,
+    source_ref,
+    decay_ref,
+    cum_ref,
+    end_ref,
+    weights_hbm,
+    gain_hbm,
+    values_hbm,
+    *refs,
 ):
     count = len(pieces)
     outs_hbm, far_ref, gain_ref = refs[:count], refs[count], refs[count + 1]
-    table_ref, reader_ref, weights_ref, weight_sems, gain_sems = refs[count + 2 : count + 7]
-    outs, out_sems = refs[count + 7 : -1], refs[-1]
+    state_refs, refs = refs[count + 2 : count + 2 + own_splits], refs[count + 2 + own_splits :]
+    table_ref, reader_ref, weights_ref, values_ref, own_ref, weight_sems, gain_sems, value_sem = refs[:8]
+    outs, out_sems = refs[8:-1], refs[-1]
+    value_copy = start_half(values_hbm, values_ref, value_sem, 1, half_order(swap)[0])
     copies = start_halves(weights_hbm, weights_ref, weight_sems, 1, swap)
     copies += start_halves(gain_hbm, gain_ref, gain_sems, 1, swap)
     tokens = queries_ref.shape[0]
     near_levels, heads, _ = decay_ref.shape
-    head_size = turned_ref.shape[0] // heads
+    head_size = 2 * other_ref.shape[0] // heads
     blocks = tokens // LANES
     row = lax.broadcasted_iota(jnp.int32, (LANES, LANES), 0)
     col = lax.broadcasted_iota(jnp.int32, (LANES, LANES), 1)
@@ -185,13 +204,23 @@
     for slot in range(far_ref.shape[0]):
         far_ref[slot] = weights_ref[near_levels + slot].astype(f32) * weight_unit * own_decay
 
+    value_copy.wait()
+    own_ref[...] = values_ref[...].T
+    row = 0
+    for state_ref in state_refs:
+        rows = state_ref.shape[0]
+        state_ref[...] = decayed_state(
+            own_ref, end_ref[...], keys_ref[...], row // head_size, rows // head_size, 0
+        )
+        row += rows
     stores = []
     for c, ((first, size), out) in enumerate(zip(pieces, outs)):
 
         def scaled(level, low, high):
             parts = []
             for h in range(first, first + size):
-                part = turned_ref[pl.ds(head_size * h, head_size), low:high].astype(f32)
+                turned_ref, place = (own_ref, h) if h < heads // 2 else (other_ref, h - heads // 2)
+                part = turned_ref[pl.ds(head_size * place, head_size), low:high].astype(f32)
                 parts.append((part * source_ref[level, h : h + 1, low:high]).astype(bf16))
             piece = jnp.concatenate(parts, axis=0)
             return jnp.concatenate([piece, piece], axis=1)
@@ -227,42 +256,62 @@
         store.wait()
 
 
-def finish_kernel(piece, swap, far_count, *refs):
-    first, size = piece
-    near_hbm, queries_ref, factor_ref, gain_ref = refs[:4]
+def finish_kernel(pieces, swap, far_count, far_rows, done_count, stores_all, *refs):
+    first, size = pieces[-1]
+    near_ref, queries_ref, factor_ref, gain_ref = refs[:4]
     far_refs, gap_refs = refs[4 : 4 + far_count], refs[4 + far_count : 4 + 2 * far_count]
-    out_hbm, out_ref, near_ref, sems = refs[-4:]
-    load = pltpu.make_async_copy(near_hbm, near_ref, sems.at[0])
-    load.start()
     rows, tokens = near_ref.shape
     heads = factor_ref.shape[1]
     head_size = rows // size
+    stores = []
+
+    def store(piece, source, target, sem):
+        half = heads // 2
+        column = half_order(swap)[piece[0] // half] * (half * head_size) + (piece[0] % half) * head_size
+        if not isinstance(column, int):
+            column = pl.multiple_of(column, LANES)
+        copy = pltpu.make_async_copy(source, target.at[:, pl.ds(column, piece[1] * head_size)], sem)
+        copy.start()
+        stores.append(copy)
+
+    out_ref = refs[4 + 2 * far_count]
+    if stores_all:
+        done_refs = refs[4 + 2 * far_count : 4 + 2 * far_count + done_count]
+        out_hbm, out_ref, sems = refs[-3:]
+        for c, done in enumerate(done_refs):
+            store(pieces[c], done, out_hbm, sems.at[c])
     queries = queries_ref[...]
     doubled = jnp.concatenate([queries, queries], axis=1)
-    combined = [0.0] * size
-    for slot in range(far_count):
-        product = contract_last(jnp.concatenate(split_two(far_refs[slot][:rows, :]), axis=1), doubled)
-        gap = jnp.exp(gap_refs[slot][first : first + size, :])
-        factor = factor_ref[slot, first : first + size, :] * jnp.concatenate([gap] * (tokens // LANES), axis=1)
-        for i in range(size):
-            combined[i] = combined[i] + factor[i : i + 1] * product[head_size * i : head_size * (i + 1)]
+    stacked = jnp.concatenate(
+        [
+            jnp.concatenate(split_two(far[row : row + rows, :]), axis=1)
+            for far, row in zip(far_refs, far_rows)
+        ],
+        axis=0,
+    )
+    products = contract_last(stacked, doubled)
     low = first * head_size
     gain = jnp.broadcast_to(gain_ref[0:1, low : low + rows], (LANES, rows)).T
-    load.wait()
+    factors = []
+    for slot in range(far_count):
+        gap = jnp.exp(gap_refs[slot][first : first + size, :])
+        factors.append(
+            factor_ref[slot, first : first + size, :] * jnp.concatenate([gap] * (tokens // LANES), axis=1)
+        )
     parts = []
     for i in range(size):
-        y = combined[i] + near_ref[head_size * i : head_size * (i + 1), :]
+        y = near_ref[head_size * i : head_size * (i + 1), :]
+        for slot in range(far_count):
+            start = rows * slot + head_size * i
+            y = y + factors[slot][i : i + 1] * products[start : start + head_size]
         inverse = lax.rsqrt(jnp.sum(y * y, axis=0, keepdims=True) * (1.0 / head_size) + norm_epsilon)
         own_gain = jnp.concatenate([gain[head_size * i : head_size * (i + 1)]] * (tokens // LANES), axis=1)
         parts.append((y * inverse * own_gain).astype(bf16))
     out_ref[...] = jnp.concatenate(parts, axis=0).T
-    half = heads // 2
-    column = half_order(swap)[first // half] * (half * head_size) + (first % half) * head_size
-    if not isinstance(column, int):
-        column = pl.multiple_of(column, LANES)
-    store = pltpu.make_async_copy(out_ref, out_hbm.at[:, pl.ds(column, rows)], sems.at[1])
-    store.start()
-    store.wait()
+    if stores_all:
+        store(pieces[-1], out_ref, out_hbm, sems.at[done_count])
+    for copy in stores:
+        copy.wait()
 
 
 vmem = functools.partial(pl.BlockSpec, memory_space=pltpu.VMEM)
@@ -286,6 +335,10 @@
 
 def one_way(bases, low):
     return [(b + low, b + low + 1) for b in bases]
+
+
+def apart(x):
+    return lax.optimization_barrier(x)
 
 
 def exchange_all(states, total, pieces, head_size):
@@ -303,7 +356,7 @@
         for c, (first, size) in enumerate(pieces):
             partner = lax.ppermute(aggregates[c], "tok", pairs)
             factor = spread(decay[first : first + size], head_size)
-            far[c].append(partner)
+            far[c].append((partner, 0))
             aggregates[c] = jnp.where(upper, factor * partner + aggregates[c], factor * aggregates[c] + partner)
         gaps.append(jnp.where(upper, prefix, masked_out))
         prefix = jnp.where(upper, prefix + partner_total, prefix)
@@ -319,43 +372,46 @@
                 carried = carried + lax.ppermute(
                     factor * carried, "seq", [(b + half + step - 1, b + half + step) for b in bases]
                 )
-            far[c].append(carried)
+            far[c].append((carried, 0))
             aggregates[c] = aggregates[c] + factor * carried
         gaps.append(prefix)
     return far, gaps
 
 
 def exchange_halves(states, total, pieces, head_size):
+    own_states, *given = states
     seq_count = lax.axis_size("seq")
     seq_bits = seq_count.bit_length() - 1
     upper = lax.axis_index("tok") == 1
     seq_index = lax.axis_index("seq")
     swap = [(0, 1), (1, 0)]
     count = len(pieces) // 2
-    heads = total.shape[0]
-    half_heads = heads // 2
+    half_heads = total.shape[0] // 2
     far = [[] for _ in pieces]
     aggregates = []
     for i in range(count):
         first, size = pieces[i]
-        rows = size * head_size
-        received = lax.ppermute(states[count + i], "tok", swap)
+        low, rows = first * head_size, size * head_size
+        received = lax.ppermute(given[i], "tok", swap)
         if i == 0:
             partner_total = received[rows:]
             partner_total = jnp.concatenate([partner_total[half_heads:], partner_total[:half_heads]])
             decay = jnp.exp(jnp.where(upper, total, partner_total))
-        partner, own = received[:rows], states[i]
+        partner = received[:rows]
+        own = (apart(own_states) if i else own_states)[low : low + rows]
         factor = spread(decay[first : first + size], head_size)
-        far[i].append(partner)
+        far[i].append((received, 0))
         aggregates.append(jnp.where(upper, factor * partner + own, factor * own + partner))
+    own_copy = lax.ppermute(own_states, "tok", swap)
     for i in range(count):
-        far[count + i].append(lax.ppermute(states[i], "tok", swap))
+        far[count + i].append((own_copy, pieces[i][0] * head_size))
     prefix = jnp.where(upper, partner_total, 0.0)
     gaps = [jnp.where(upper, jnp.zeros_like(total), masked_out)]
     group_decay = jnp.exp(total + partner_total)
     for place in range(seq_bits):
         half = 1 << place
         bases = range(0, seq_count, 2 * half)
+        levels = []
         for i in range(count):
             first, size = pieces[i]
             factor = spread(group_decay[first : first + size], head_size)
@@ -364,9 +420,15 @@
             for step in range(1, half):
                 arrived = lax.ppermute(factor * carried, "seq", one_way(bases, half + step - 1))
                 carried = jnp.where(seq_index % (2 * half) == half + step, arrived, carried)
-            far[i].append(carried)
-            far[count + i].append(lax.ppermute(carried, "tok", swap))
+            far[i].append((carried, 0))
+            levels.append(carried)
+            if place + 1 == seq_bits:
+                far[count + i].append((lax.ppermute(carried, "tok", swap), 0))
             aggregates[i] = aggregates[i] + factor * carried
+        if place + 1 < seq_bits:
+            shared = lax.ppermute(jnp.concatenate(levels), "tok", swap)
+            for i in range(count):
+                far[count + i].append((shared, pieces[i][0] * head_size))
         gaps.append(jnp.where((seq_index >> place) & 1 == 1, prefix, masked_out))
     return far, gaps
 
@@ -380,87 +442,107 @@
     far_count = lax.axis_size("tok").bit_length() + lax.axis_size("seq").bit_length() - 2
     swap = lax.axis_size("tok") == 2
     half = heads // 2
-    count = PIECES
-    size = half // count
-    pieces = [(size * i, size) for i in range(2 * count)]
-    order = [*range(count, 2 * count), *range(count)]
-    with_totals = count if swap else None
-
-    *states, total, turned, source, decay, cum, keys, queries = pl.pallas_call(
-        functools.partial(state_kernel, pieces, order, swap, with_totals),
+    count = len(PIECE_SHARES)
+    sizes = [half * share // sum(PIECE_SHARES) for share in PIECE_SHARES] * 2
+    pieces = [(sum(sizes[:i]), size) for i, size in enumerate(sizes)]
+    own_rows = [half * head_size] if swap else [n * head_size for _, n in pieces[:count]]
+
+    *given, total, other, source, decay, cum, to_end, keys, queries = pl.pallas_call(
+        functools.partial(state_kernel, pieces, swap),
         name="state",
         out_shape=[
-            jax.ShapeDtypeStruct((n * head_size + (heads if c == with_totals else 0), state_size), f32)
-            for c, (_, n) in enumerate(pieces)
+            jax.ShapeDtypeStruct((n * head_size + (heads if swap and c == 0 else 0), state_size), f32)
+            for c, (_, n) in enumerate(pieces[count:])
         ]
         + [
             jax.ShapeDtypeStruct((heads, LANES), f32),
-            jax.ShapeDtypeStruct((columns, tokens), bf16),
+            jax.ShapeDtypeStruct((columns // 2, tokens), bf16),
             jax.ShapeDtypeStruct((near_levels - 1, heads, tokens), f32),
             jax.ShapeDtypeStruct((near_levels, heads, tokens), f32),
+            jax.ShapeDtypeStruct((heads, tokens), f32),
             jax.ShapeDtypeStruct((heads, tokens), f32),
             jax.ShapeDtypeStruct(key_rows.shape, key_rows.dtype),
             jax.ShapeDtypeStruct(query_rows.shape, query_rows.dtype),
         ],
         in_specs=[hbm()] * 4,
-        out_specs=[vmem()] * (len(pieces) + 7),
+        out_specs=[vmem()] * (count + 8),
         scratch_shapes=[
-            pltpu.VMEM(values.shape, values.dtype),
+            pltpu.VMEM((tokens, columns // 2), values.dtype),
             pltpu.VMEM(decay_codes.shape, decay_codes.dtype),
             dma((2,)),
-            dma((2,)),
-            dma((2,)),
+            dma((3,)),
         ],
         compiler_params=params,
     )(*(in_hbm(x) for x in (values, key_rows, query_rows, decay_codes)))
 
     near_call = pl.pallas_call(
-        functools.partial(near_kernel, pieces, swap),
+        functools.partial(near_kernel, pieces, swap, len(own_rows)),
         name="near",
         out_shape=[pltpu.HBM((n * head_size, tokens), f32) for _, n in pieces]
         + [
             jax.ShapeDtypeStruct((far_count, heads, tokens), f32),
             jax.ShapeDtypeStruct((1, columns), f32),
-        ],
-        in_specs=[vmem()] * 6 + [hbm()] * 2,
-        out_specs=[hbm()] * len(pieces) + [vmem()] * 2,
+        ]
+        + [jax.ShapeDtypeStruct((n, state_size), f32) for n in own_rows],
+        in_specs=[vmem()] * 7 + [hbm()] * 3,
+        out_specs=[hbm()] * len(pieces) + [vmem()] * (2 + len(own_rows)),
         scratch_shapes=[
             pltpu.VMEM((tokens // LANES, 2 * LANES, 2 * LANES), bf16),
             pltpu.VMEM((near_levels, heads, tokens), f32),
             pltpu.VMEM(weight_codes.shape, weight_codes.dtype),
+            pltpu.VMEM((tokens, columns // 2), values.dtype),
+            pltpu.VMEM((columns // 2, tokens), bf16),
             dma((2,)),
             dma((2,)),
+            dma(()),
         ]
         + [pltpu.VMEM((n * head_size, tokens), f32) for _, n in pieces]
         + [dma((len(pieces),))],
         compiler_params=params,
     )
-    *near, far_factor, gain = near_call(
-        turned, queries, keys, source, decay, cum, in_hbm(weight_codes), in_hbm(norm_gain.reshape(1, columns))
+    outputs = near_call(
+        other,
+        queries,
+        keys,
+        source,
+        decay,
+        cum,
+        to_end,
+        in_hbm(weight_codes),
+        in_hbm(norm_gain.reshape(1, columns)),
+        in_hbm(values),
     )
+    near, (far_factor, gain, *own_states) = outputs[: len(pieces)], outputs[len(pieces) :]
+    states = [*own_states, *given]
 
     exchange = exchange_halves if swap else exchange_all
     far, gaps = exchange(states, total, pieces, head_size)
-    out = None
+    done = []
     for c, piece in enumerate(pieces):
         rows = piece[1] * head_size
-        operands = [near[c], queries, far_factor, gain, *far[c], *gaps]
-        in_specs = [hbm()] + [vmem()] * (len(operands) - 1)
+        far_arrays, far_rows = zip(*far[c])
+        operands = [near[c], queries, far_factor, gain, *far_arrays, *gaps]
+        stores = c + 2 >= len(pieces)
+        operands += done if stores else []
+        specs = [vmem()] * len(operands)
         aliases = {}
-        if out is not None:
+        if c + 1 == len(pieces):
             aliases = {len(operands): 0}
             operands.append(out)
-            in_specs.append(hbm())
+            specs.append(hbm())
         finish_call = pl.pallas_call(
-            functools.partial(finish_kernel, piece, swap, far_count),
-            out_shape=pltpu.HBM((tokens, columns), bf16),
-            in_specs=in_specs,
-            out_specs=hbm(),
-            scratch_shapes=[pltpu.VMEM((tokens, rows), bf16), pltpu.VMEM((rows, tokens), f32), dma((2,))],
+            functools.partial(finish_kernel, pieces[: c + 1], swap, far_count, far_rows, len(done) if stores else 0, stores),
+            out_shape=pltpu.HBM((tokens, columns), bf16)
+            if stores
+            else jax.ShapeDtypeStruct((tokens, rows), bf16),
+            in_specs=specs,
+            out_specs=hbm() if stores else vmem(),
+            scratch_shapes=[pltpu.VMEM((tokens, rows), bf16), dma((len(done) + 1,))] if stores else [],
             input_output_aliases=aliases,
             compiler_params=params,
         )
         out = finish_call(*operands)
+        done = [] if stores else [*done, out]
     return out
 
 

time: 47.2 us -> 43.4 us (0.919)
  the two profiles are of different devices: /device:TPU:26 before, /device:TPU:22 now
where the time goes in v3:
time: 43.4 us; the launch traced here: 43.1 us
  waiting for transfers between devices  20.3 us (47%)
  starting transfers between devices  12.8 us (29%)
  Pallas kernels  9.21 us (21%)
  local copies, waits for them, and re-layouts  0.5 us (1%)
    ppermute x4, waiting for transfers between devices, exchange_halves(): carried = lax.ppermute(aggregates[i], 'seq', first_hop)  9.29 us
    ppermute x4, starting transfers between devices, exchange_halves(): carried = lax.ppermute(aggregates[i], 'seq', first_hop)  4.74 us
    ppermute x1, waiting for transfers between devices, exchange_halves(): shared = lax.ppermute(jnp.concatenate(levels), 'tok', swap)  4.43 us
    pallas_call x1, Pallas kernels, local(): near_call(other, queries, keys, source, decay, cum, to_end, in_hbm(weight...  3.96 us
    pallas_call x4, Pallas kernels, local(): out = finish_call(*operands)  3.68 us
    ppermute x2, starting transfers between devices, exchange_halves(): lax.ppermute(factor * carried, 'seq', one_way(bases, half + step - 1))  2.59 us
    ppermute x2, waiting for transfers between devices, exchange_halves(): received = lax.ppermute(given[i], 'tok', swap)  2.19 us
    ppermute x2, starting transfers between devices, exchange_halves(): received = lax.ppermute(given[i], 'tok', swap)  2.09 us
  transfers between devices with their start and end apart: 12, of which 9 were waited for; matrix products, arithmetic and copies ran while one was open for 0% of the time, Pallas kernels for 15%

profile of v3, /device:TPU:22, one launch (start us, length us, event | category | flops | bytes accessed | tf_op | source)
XLA Modules:
  0.0 43.1 jit_solution(15400803373435055452)
XLA Ops:
  0.0 1.6 %state.1 = (f32[272,128]{1,0:T(8,128)S(1)}, f32[256,128]{1,0:T(8,128)S(1)}, f32[16,128]{1,0:T(8,128)S(1)}, bf16[512,512]{1,0:T(8,128)(2,1)S(1)}, f32[3,16,512]{2...) custom-call(bf16[512,1024]{1,0:T(8,128)(2,1)} %values_hbm.3, ...), custom_call_target="tpu_custom_call" | custom-call | tf_op jit(solution)/shard_map/state/pallas_call | solution.py:450
  1.6 0.6 %collective-permute-start.1 = (f32[272,128]{1,0:T(8,128)S(1)}, f32[272,128]{1,0:T(8,128)S(1)}, u32[]{:S(2)}, u32[]{:S(2)}) collective-permute-start(f32[272,128]{1,0:T(8,128)S(1)} %get-tuple-element.34), channel_id=1, source_target_pairs={{0,2},{2,0},{1,3},{3,1},{4,6},{6,4},{5,7},{7,5},{8,10},{10,8},{9,1... | collective-permute-start | bytes 417800 | tf_op jit(solution)/shard_map/ppermute | solution.py:395
  2.2 1.5 %collective-permute-start.3 = (f32[256,128]{1,0:T(8,128)S(1)}, f32[256,128]{1,0:T(8,128)S(1)}, u32[]{:S(2)}, u32[]{:S(2)}) collective-permute-start(f32[256,128]{1,0:T(8,128)S(1)} %get-tuple-element.35), channel_id=1, source_target_pairs={{0,2},{2,0},{1,3},{3,1},{4,6},{6,4},{5,7},{7,5},{8,10},{10,8},{9,1... | collective-permute-start | bytes 393224 | tf_op jit(solution)/shard_map/ppermute | solution.py:395
  3.7 4.0 %near.1 = (f32[256,512]{1,0:T(8,128)}, f32[256,512]{1,0:T(8,128)}, f32[256,512]{1,0:T(8,128)}, f32[256,512]{1,0:T(8,128)}, f32[3,16,512]{2,1,0:T(8,128)S(1)}, /*...) custom-call(bf16[512,512]{1,0:T(8,128)(2,1)S(1)} %get-tuple-element.22.other_ref, ...), custom_call_target="tpu_custom_call" | custom-call | tf_op jit(solution)/shard_map/near/pallas_call | solution.py:503
  7.6 0.5 %collective-permute-done.1.refs_4_ = f32[272,128]{1,0:T(8,128)S(1)} collective-permute-done((f32[272,128]{1,0:T(8,128)S(1)}, f32[272,128]{1,0:T(8,128)S(1)}, u32[]{:S(2)}, u32[]{:S(2)}) %collective-permute-start.1) | collective-permute-done | bytes 139296 | tf_op jit(solution)/shard_map/ppermute | solution.py:395
  8.2 1.7 %collective-permute-done.3.refs_4_ = f32[256,128]{1,0:T(8,128)S(1)} collective-permute-done((f32[256,128]{1,0:T(8,128)S(1)}, f32[256,128]{1,0:T(8,128)S(1)}, u32[]{:S(2)}, u32[]{:S(2)}) %collective-permute-start.3) | collective-permute-done | bytes 131104 | tf_op jit(solution)/shard_map/ppermute | solution.py:395
  9.9 1.6 %collective-permute-start.4 = (f32[256,128]{1,0:T(8,128)S(1)}, f32[256,128]{1,0:T(8,128)S(1)}, u32[]{:S(2)}, u32[]{:S(2)}) collective-permute-start(f32[256,128]{1,0:T(8,128)S(1)} %fusion.4), channel_id=1, source_target_pairs={{0,4},{4,0},{8,12},{12,8},{1,5},{5,1},{9,13},{13,9},{2,6},{6,2},{1... | collective-permute-start | bytes 393224 | tf_op jit(solution)/shard_map/ppermute | solution.py:419
  11.6 0.5 %collective-permute-start.2 = (f32[256,128]{1,0:T(8,128)S(1)}, f32[256,128]{1,0:T(8,128)S(1)}, u32[]{:S(2)}, u32[]{:S(2)}) collective-permute-start(f32[256,128]{1,0:T(8,128)S(1)} %fusion.1), channel_id=1, source_target_pairs={{0,4},{4,0},{8,12},{12,8},{1,5},{5,1},{9,13},{13,9},{2,6},{6,2},{1... | collective-permute-start | bytes 393224 | tf_op jit(solution)/shard_map/ppermute | solution.py:419
  12.1 5.1 %collective-permute-done.2.refs_5_ = f32[256,128]{1,0:T(8,128)S(1)} collective-permute-done((f32[256,128]{1,0:T(8,128)S(1)}, f32[256,128]{1,0:T(8,128)S(1)}, u32[]{:S(2)}, u32[]{:S(2)}) %collective-permute-start.2) | collective-permute-done | bytes 131104 | tf_op jit(solution)/shard_map/ppermute | solution.py:419
  17.2 1.3 %collective-permute-start.9 = (f32[256,128]{1,0:T(8,128)S(1)}, f32[256,128]{1,0:T(8,128)S(1)}, u32[]{:S(2)}, u32[]{:S(2)}) collective-permute-start(f32[256,128]{1,0:T(8,128)S(1)} %fusion.7), channel_id=1, source_target_pairs={{4,8},{5,9},{6,10},{7,11},{20,24},{21,25},{22,26},{23,27}} | collective-permute-start | bytes 393224 | tf_op jit(solution)/shard_map/ppermute | solution.py:419
  18.5 0.0 collective-permute-done.4.refs_5_
  18.5 1.3 %collective-permute-start.6 = (f32[256,128]{1,0:T(8,128)S(1)}, f32[256,128]{1,0:T(8,128)S(1)}, u32[]{:S(2)}, u32[]{:S(2)}) collective-permute-start(f32[256,128]{1,0:T(8,128)S(1)} %fusion.6), channel_id=1, source_target_pairs={{4,8},{5,9},{6,10},{7,11},{20,24},{21,25},{22,26},{23,27}} | collective-permute-start | bytes 393224 | tf_op jit(solution)/shard_map/ppermute | solution.py:419
  19.8 4.2 %collective-permute-done.9 = f32[256,128]{1,0:T(8,128)S(1)} collective-permute-done((f32[256,128]{1,0:T(8,128)S(1)}, f32[256,128]{1,0:T(8,128)S(1)}, u32[]{:S(2)}, u32[]{:S(2)}) %collective-permute-start.9) | collective-permute-done | bytes 131104 | tf_op jit(solution)/shard_map/ppermute | solution.py:419
  24.0 1.3 %collective-permute-start.10 = (f32[256,128]{1,0:T(8,128)S(1)}, f32[256,128]{1,0:T(8,128)S(1)}, u32[]{:S(2)}, u32[]{:S(2)}) collective-permute-start(f32[256,128]{1,0:T(8,128)S(1)} %bitcast_multiply_fusion), channel_id=1, source_target_pairs={{8,12},{9,13},{10,14},{11,15},{24,28},{25,29},{26,30},{27,31}} | collective-permute-start | bytes 393224 | tf_op jit(solution)/shard_map/ppermute | solution.py:421
  25.4 0.6 %collective-permute-start = (f32[512,128]{1,0:T(8,128)S(1)}, f32[512,128]{1,0:T(8,128)S(1)}, u32[]{:S(2)}, u32[]{:S(2)}) collective-permute-start(f32[512,128]{1,0:T(8,128)S(1)} %get-tuple-element.32), channel_id=1, source_target_pairs={{0,2},{2,0},{1,3},{3,1},{4,6},{6,4},{5,7},{7,5},{8,10},{10,8},{9,1... | collective-permute-start | bytes 786440 | tf_op jit(solution)/shard_map/ppermute | solution.py:405
  26.0 0.0 copy-start.3
  26.0 1.6 %collective-permute-start.5 = (f32[512,128]{1,0:T(8,128)S(1)}, f32[512,128]{1,0:T(8,128)S(1)}, u32[]{:S(2)}, u32[]{:S(2)}) collective-permute-start(f32[512,128]{1,0:T(8,128)S(1)} %pad_maximum_fusion), channel_id=1, source_target_pairs={{0,2},{2,0},{1,3},{3,1},{4,6},{6,4},{5,7},{7,5},{8,10},{10,8},{9,1... | collective-permute-start | bytes 786440 | tf_op jit(solution)/shard_map/ppermute | solution.py:429
  27.5 0.0 collective-permute-done.6
  27.6 1.3 %collective-permute-start.7 = (f32[256,128]{1,0:T(8,128)S(1)}, f32[256,128]{1,0:T(8,128)S(1)}, u32[]{:S(2)}, u32[]{:S(2)}) collective-permute-start(f32[256,128]{1,0:T(8,128)S(1)} %bitcast_multiply_fusion.2), channel_id=1, source_target_pairs={{8,12},{9,13},{10,14},{11,15},{24,28},{25,29},{26,30},{27,31}} | collective-permute-start | bytes 393224 | tf_op jit(solution)/shard_map/ppermute | solution.py:421
  28.9 0.0 collective-permute-done.10
  28.9 0.6 %collective-permute-start.11 = (f32[256,128]{1,0:T(8,128)S(1)}, f32[256,128]{1,0:T(8,128)S(1)}, u32[]{:S(2)}, u32[]{:S(2)}) collective-permute-start(f32[256,128]{1,0:T(8,128)S(1)} %broadcast_select_fusion.refs_6_), channel_id=1, source_target_pairs={{0,2},{2,0},{1,3},{3,1},{4,6},{6,4},{5,7},{7,5},{8,10},{10,8},{9,1... | collective-permute-start | bytes 393224 | tf_op jit(solution)/shard_map/ppermute | solution.py:426
  29.5 1.9 %collective-permute-done.7 = f32[256,128]{1,0:T(8,128)S(1)} collective-permute-done((f32[256,128]{1,0:T(8,128)S(1)}, f32[256,128]{1,0:T(8,128)S(1)}, u32[]{:S(2)}, u32[]{:S(2)}) %collective-permute-start.7) | collective-permute-done | bytes 131104 | tf_op jit(solution)/shard_map/ppermute | solution.py:421
  31.4 0.6 %collective-permute-start.8 = (f32[256,128]{1,0:T(8,128)S(1)}, f32[256,128]{1,0:T(8,128)S(1)}, u32[]{:S(2)}, u32[]{:S(2)}) collective-permute-start(f32[256,128]{1,0:T(8,128)S(1)} %broadcast_select_fusion.1.refs_6_), channel_id=1, source_target_pairs={{0,2},{2,0},{1,3},{3,1},{4,6},{6,4},{5,7},{7,5},{8,10},{10,8},{9,1... | collective-permute-start | bytes 393224 | tf_op jit(solution)/shard_map/ppermute | solution.py:426
  32.0 0.0 copy-done.3
  32.0 0.0 copy-start.2
  32.0 0.6 %shard_map.65.refs_11_ = bf16[512,256]{1,0:T(8,128)(2,1)S(1)} custom-call(f32[256,512]{1,0:T(8,128)S(1)} %copy-done.3, bf16[512,128]{1,0:T(8,128)(2,1)S(1)} %get-tuple-element.23.queries_ref.refs_1_, f32[3,16,512]{2,1,0:T(8,128)S(1)} %get-tuple-element.30.refs_2_, f32[1,1024]{1,0:T(1,128)S(1)} %get-tuple-element.31.refs_3_, ...), custom_call_target="tpu_custom_call" | custom-call | tf_op jit(solution)/shard_map/pallas_call | solution.py:544
  32.5 0.5 %copy-done.2 = f32[256,512]{1,0:T(8,128)S(1)} copy-done((f32[256,512]{1,0:T(8,128)S(1)}, f32[256,512]{1,0:T(8,128)}, u32[]{:S(2)}) %copy-start.2) | copy-done | bytes 524312
  33.0 0.0 copy-start.1
  33.0 0.6 %shard_map.64.refs_10_ = bf16[512,256]{1,0:T(8,128)(2,1)S(1)} custom-call(f32[256,512]{1,0:T(8,128)S(1)} %copy-done.2, bf16[512,128]{1,0:T(8,128)(2,1)S(1)} %get-tuple-element.23.queries_ref.refs_1_, f32[3,16,512]{2,1,0:T(8,128)S(1)} %get-tuple-element.30.refs_2_, f32[1,1024]{1,0:T(1,128)S(1)} %get-tuple-element.31.refs_3_, ...), custom_call_target="tpu_custom_call" | custom-call | tf_op jit(solution)/shard_map/pallas_call | solution.py:544
  33.6 1.0 %collective-permute-done.refs_4_ = f32[512,128]{1,0:T(8,128)S(1)} collective-permute-done((f32[512,128]{1,0:T(8,128)S(1)}, f32[512,128]{1,0:T(8,128)S(1)}, u32[]{:S(2)}, u32[]{:S(2)}) %collective-permute-start) | collective-permute-done | bytes 262176 | tf_op jit(solution)/shard_map/ppermute | solution.py:405
  34.6 4.4 %collective-permute-done.5.refs_5_ = f32[512,128]{1,0:T(8,128)S(1)} collective-permute-done((f32[512,128]{1,0:T(8,128)S(1)}, f32[512,128]{1,0:T(8,128)S(1)}, u32[]{:S(2)}, u32[]{:S(2)}) %collective-permute-start.5) | collective-permute-done | bytes 262176 | tf_op jit(solution)/shard_map/ppermute | solution.py:429
  39.0 1.4 %collective-permute-done.11.refs_6_ = f32[256,128]{1,0:T(8,128)S(1)} collective-permute-done((f32[256,128]{1,0:T(8,128)S(1)}, f32[256,128]{1,0:T(8,128)S(1)}, u32[]{:S(2)}, u32[]{:S(2)}) %collective-permute-start.11) | collective-permute-done | bytes 131104 | tf_op jit(solution)/shard_map/ppermute | solution.py:426
  40.4 0.0 copy-done.1
  40.4 0.0 copy-start
  40.4 1.3 %shard_map.66.refs_10_ = bf16[512,1024]{1,0:T(8,128)(2,1)} custom-call(f32[256,512]{1,0:T(8,128)S(1)} %copy-done.1, bf16[512,128]{1,0:T(8,128)(2,1)S(1)} %get-tuple-element.23.queries_ref.refs_1_, f32[3,16,512]{2,1,0:T(8,128)S(1)} %get-tuple-element.30.refs_2_, f32[1,1024]{1,0:T(1,128)S(1)} %get-tuple-element.31.refs_3_, ...), custom_call_target="tpu_custom_call" | custom-call | tf_op jit(solution)/shard_map/pallas_call | solution.py:544
  41.7 0.1 collective-permute-done.8.refs_6_
  41.8 0.0 copy-done
  41.8 1.3 %shard_map.67 = bf16[512,1024]{1,0:T(8,128)(2,1)} custom-call(f32[256,512]{1,0:T(8,128)S(1)} %copy-done, bf16[512,128]{1,0:T(8,128)(2,1)S(1)} %get-tuple-element.23.queries_ref.refs_1_, f32[3,16,512]{2,1,0:T(8,128)S(1)} %get-tuple-element.30.refs_2_, f32[1,1024]{1,0:T(1,128)S(1)} %get-tuple-element.31.refs_3_, ...), custom_call_target="tpu_custom_call", output_to_operand_aliasing={{}: (10, {})} | custom-call | tf_op jit(solution)/shard_map/pallas_call | solution.py:544
  (14 shorter events, 0.2 us)
Async XLA Ops:
  1.6 6.6 %collective-permute-start.1 = (f32[272,128]{1,0:T(8,128)S(1)}, f32[272,128]{1,0:T(8,128)S(1)}, u32[]{:S(2)}, u32[]{:S(2)}) collective-permute-start(f32[272,128]{1,0:T(8,128)S(1)} %get-tuple-element.34), channel_id=1, source_target_pairs={{0,2},{2,0},{1,3},{3,1},{4,6},{6,4},{5,7},{7,5},{8,10},{10,8},{9,1... | collective-permute-start | bytes 417800 | tf_op jit(solution)/shard_map/ppermute | solution.py:395
  2.2 7.7 %collective-permute-start.3 = (f32[256,128]{1,0:T(8,128)S(1)}, f32[256,128]{1,0:T(8,128)S(1)}, u32[]{:S(2)}, u32[]{:S(2)}) collective-permute-start(f32[256,128]{1,0:T(8,128)S(1)} %get-tuple-element.35), channel_id=1, source_target_pairs={{0,2},{2,0},{1,3},{3,1},{4,6},{6,4},{5,7},{7,5},{8,10},{10,8},{9,1... | collective-permute-start | bytes 393224 | tf_op jit(solution)/shard_map/ppermute | solution.py:395
  9.9 8.6 %collective-permute-start.4 = (f32[256,128]{1,0:T(8,128)S(1)}, f32[256,128]{1,0:T(8,128)S(1)}, u32[]{:S(2)}, u32[]{:S(2)}) collective-permute-start(f32[256,128]{1,0:T(8,128)S(1)} %fusion.4), channel_id=1, source_target_pairs={{0,4},{4,0},{8,12},{12,8},{1,5},{5,1},{9,13},{13,9},{2,6},{6,2},{1... | collective-permute-start | bytes 393224 | tf_op jit(solution)/shard_map/ppermute | solution.py:419
  11.6 5.6 %collective-permute-start.2 = (f32[256,128]{1,0:T(8,128)S(1)}, f32[256,128]{1,0:T(8,128)S(1)}, u32[]{:S(2)}, u32[]{:S(2)}) collective-permute-start(f32[256,128]{1,0:T(8,128)S(1)} %fusion.1), channel_id=1, source_target_pairs={{0,4},{4,0},{8,12},{12,8},{1,5},{5,1},{9,13},{13,9},{2,6},{6,2},{1... | collective-permute-start | bytes 393224 | tf_op jit(solution)/shard_map/ppermute | solution.py:419
  17.2 6.9 %collective-permute-start.9 = (f32[256,128]{1,0:T(8,128)S(1)}, f32[256,128]{1,0:T(8,128)S(1)}, u32[]{:S(2)}, u32[]{:S(2)}) collective-permute-start(f32[256,128]{1,0:T(8,128)S(1)} %fusion.7), channel_id=1, source_target_pairs={{4,8},{5,9},{6,10},{7,11},{20,24},{21,25},{22,26},{23,27}} | collective-permute-start | bytes 393224 | tf_op jit(solution)/shard_map/ppermute | solution.py:419
  18.5 9.0 %collective-permute-start.6 = (f32[256,128]{1,0:T(8,128)S(1)}, f32[256,128]{1,0:T(8,128)S(1)}, u32[]{:S(2)}, u32[]{:S(2)}) collective-permute-start(f32[256,128]{1,0:T(8,128)S(1)} %fusion.6), channel_id=1, source_target_pairs={{4,8},{5,9},{6,10},{7,11},{20,24},{21,25},{22,26},{23,27}} | collective-permute-start | bytes 393224 | tf_op jit(solution)/shard_map/ppermute | solution.py:419
  24.0 4.8 %collective-permute-start.10 = (f32[256,128]{1,0:T(8,128)S(1)}, f32[256,128]{1,0:T(8,128)S(1)}, u32[]{:S(2)}, u32[]{:S(2)}) collective-permute-start(f32[256,128]{1,0:T(8,128)S(1)} %bitcast_multiply_fusion), channel_id=1, source_target_pairs={{8,12},{9,13},{10,14},{11,15},{24,28},{25,29},{26,30},{27,31}} | collective-permute-start | bytes 393224 | tf_op jit(solution)/shard_map/ppermute | solution.py:421
  25.4 9.2 %collective-permute-start = (f32[512,128]{1,0:T(8,128)S(1)}, f32[512,128]{1,0:T(8,128)S(1)}, u32[]{:S(2)}, u32[]{:S(2)}) collective-permute-start(f32[512,128]{1,0:T(8,128)S(1)} %get-tuple-element.32), channel_id=1, source_target_pairs={{0,2},{2,0},{1,3},{3,1},{4,6},{6,4},{5,7},{7,5},{8,10},{10,8},{9,1... | collective-permute-start | bytes 786440 | tf_op jit(solution)/shard_map/ppermute | solution.py:405
  26.0 6.0 %copy-start.3 = (f32[256,512]{1,0:T(8,128)S(1)}, f32[256,512]{1,0:T(8,128)}, u32[]{:S(2)}) copy-start(f32[256,512]{1,0:T(8,128)} %get-tuple-element.38.refs_0_) | copy-start | bytes 1572868
  26.0 13.1 %collective-permute-start.5 = (f32[512,128]{1,0:T(8,128)S(1)}, f32[512,128]{1,0:T(8,128)S(1)}, u32[]{:S(2)}, u32[]{:S(2)}) collective-permute-start(f32[512,128]{1,0:T(8,128)S(1)} %pad_maximum_fusion), channel_id=1, source_target_pairs={{0,2},{2,0},{1,3},{3,1},{4,6},{6,4},{5,7},{7,5},{8,10},{10,8},{9,1... | collective-permute-start | bytes 786440 | tf_op jit(solution)/shard_map/ppermute | solution.py:429
  27.6 3.8 %collective-permute-start.7 = (f32[256,128]{1,0:T(8,128)S(1)}, f32[256,128]{1,0:T(8,128)S(1)}, u32[]{:S(2)}, u32[]{:S(2)}) collective-permute-start(f32[256,128]{1,0:T(8,128)S(1)} %bitcast_multiply_fusion.2), channel_id=1, source_target_pairs={{8,12},{9,13},{10,14},{11,15},{24,28},{25,29},{26,30},{27,31}} | collective-permute-start | bytes 393224 | tf_op jit(solution)/shard_map/ppermute | solution.py:421
  28.9 11.5 %collective-permute-start.11 = (f32[256,128]{1,0:T(8,128)S(1)}, f32[256,128]{1,0:T(8,128)S(1)}, u32[]{:S(2)}, u32[]{:S(2)}) collective-permute-start(f32[256,128]{1,0:T(8,128)S(1)} %broadcast_select_fusion.refs_6_), channel_id=1, source_target_pairs={{0,2},{2,0},{1,3},{3,1},{4,6},{6,4},{5,7},{7,5},{8,10},{10,8},{9,1... | collective-permute-start | bytes 393224 | tf_op jit(solution)/shard_map/ppermute | solution.py:426
  31.4 10.5 %collective-permute-start.8 = (f32[256,128]{1,0:T(8,128)S(1)}, f32[256,128]{1,0:T(8,128)S(1)}, u32[]{:S(2)}, u32[]{:S(2)}) collective-permute-start(f32[256,128]{1,0:T(8,128)S(1)} %broadcast_select_fusion.1.refs_6_), channel_id=1, source_target_pairs={{0,2},{2,0},{1,3},{3,1},{4,6},{6,4},{5,7},{7,5},{8,10},{10,8},{9,1... | collective-permute-start | bytes 393224 | tf_op jit(solution)/shard_map/ppermute | solution.py:426
  32.0 1.0 %copy-start.2 = (f32[256,512]{1,0:T(8,128)S(1)}, f32[256,512]{1,0:T(8,128)}, u32[]{:S(2)}) copy-start(f32[256,512]{1,0:T(8,128)} %get-tuple-element.37.refs_0_) | copy-start | bytes 1572868
  33.0 7.4 %copy-start.1 = (f32[256,512]{1,0:T(8,128)S(1)}, f32[256,512]{1,0:T(8,128)}, u32[]{:S(2)}) copy-start(f32[256,512]{1,0:T(8,128)} %get-tuple-element.36.refs_0_) | copy-start | bytes 1572868
  40.4 1.4 %copy-start = (f32[256,512]{1,0:T(8,128)S(1)}, f32[256,512]{1,0:T(8,128)}, u32[]{:S(2)}) copy-start(f32[256,512]{1,0:T(8,128)} %get-tuple-element.29.refs_0_) | copy-start | bytes 1572868
